TPU v7x, 256 devices: a 8x8x2 block of a 8x8x16 slice. The times are simulated.
256 devices in a mesh: grp: 2 (over z), dap: 128 (over y, x, core).
Axes of the slice: x: 8, y: 8, z: 2, core: 2. Of those that a mesh axis runs over, the one named last changes fastest.
The devices are a block of a 8x8x16 slice.
Arguments:
- homolog_stack_tensor: bfloat16 [512, 512, 256], P(('grp', 'dap')), parts along dimension 0, may hold values from -6.5 to 6.5
- occupancy_indicator: int32 [512, 512], P('grp'), parts along dimension 0, may hold values from 0 to 1, as said below
- chain_existence_flags: int32 [512], P('grp'), parts along dimension 0, may hold values from 0 to 1, as said below
- focus_normal_factor: float32 [256], replicated, may hold values from 0.25 to 1.75
- focus_normal_addend: float32 [256], replicated, may hold values from -3 to 3
- probe_index_weights: bfloat16 [256, 512], replicated, may hold values from -3 to 3
- payload_valve_weights: bfloat16 [256, 512], replicated, may hold values from -0.375 to 0.375
- logistic_valve_addend: float32 [256], replicated, may hold values from -4 to 4
- focus_exit_weights: bfloat16 [256, 256], replicated, may hold values from -0.375 to 0.375
- focus_exit_addend: float32 [256], replicated, may hold values from -3 to 3
- product_mean_layer_stretch: float32 [256], replicated, may hold values from 0.25 to 1.75
- product_mean_layer_shift: float32 [256], replicated, may hold values from -2 to 2
- twin_map_matrix: bfloat16 [256, 64], replicated, may hold values from -0.375 to 0.375
- twin_map_shift: float32 [64], replicated, may hold values from -2 to 2
- couple_map_matrix: bfloat16 [1024, 128], replicated, may hold values from -0.75 to 0.75
- couple_map_shift: float32 [128], replicated, may hold values from -3 to 3
Outputs:
- alignment_after: bfloat16 [512, 512, 256], P('grp', 'dap'), parts along dimension 0
- pair_features_after: bfloat16 [1024, 512, 128], P(('grp', 'dap')), parts along dimension 0
There are 2 independent parts, one for each index of `grp`. A program takes and returns all parts, laid end to end along the dimension named above; an argument that names none is the same for every part. Nothing has to cross between parts.
Inputs may be any that keep to these rules, and one draw needn't show every extreme that they name: `chain_existence_flags`: 1 for the first 128 sequences, 0 for the last one. `occupancy_indicator`: every sequence is 0 from some residue on (the last residue always, never more than the last 256); before it sequence 0 is all 1 and the others have gaps.
All inputs are finite; a program needn't handle non-finite values.
Results may differ from a plain program's by a relative error of at most 0.008.
Values may be sent and summed in bfloat16 or wider, within the bound.
A program may use at most 64 MiB of HBM per device.

v0:
```python
import jax
import jax.numpy as jnp
from jax import lax
from jax.sharding import Mesh
from jax.sharding import PartitionSpec as P

HEAD_COUNT = 8
HEAD_CHANNELS = 32
OUTER_CHANNELS = 32
PAIR_DIM = 128
DAP = ("dap_0", "dap_1", "dap_2")
GRP_DAP = ("grp", "dap_0", "dap_1", "dap_2")


EPSILON = 1e-05
MASKED = -100000.0


def in_blocks(value, dim, count):
    shape = value.shape
    parts = value.reshape(*shape[:dim], count, shape[dim] // count, *shape[dim + 1 :])
    return jnp.moveaxis(parts, dim, 0)


def joined_along(parts, dim):
    parts = jnp.moveaxis(parts, 0, dim)
    shape = parts.shape
    return parts.reshape(*shape[:dim], shape[dim] * shape[dim + 1], *shape[dim + 2 :])


def exchange_in_order(parts, axes, turns):
    shape = [lax.axis_size(a) for a in axes]
    parts = parts.reshape(*shape, *parts.shape[1:])
    for k in turns:
        parts = lax.all_to_all(parts, axes[k], split_axis=k, concat_axis=k, tiled=True)
    return parts.reshape(-1, *parts.shape[len(axes) :])


def exchange_by_chip(value, groups, turns, split_dim, concat_dim):
    count = lax.axis_size(groups[0]) * lax.axis_size(groups[1])
    parts = in_blocks(value, split_dim, count)
    return joined_along(exchange_in_order(parts, groups, turns), concat_dim)


def layer_norm(value_vectors, scale_vec, shift_vec):
    widened = value_vectors.astype(jnp.float32)
    centred = widened - jnp.mean(widened, axis=-1, keepdims=True)
    variance = jnp.mean(centred * centred, axis=-1, keepdims=True)
    scaled = centred * lax.rsqrt(variance + EPSILON)
    return (scaled * scale_vec + shift_vec).astype(jnp.bfloat16)


def heed_across_lanes(
    vertical_pieces,
    present_mask,
    focus_normal_factor,
    focus_normal_addend,
    probe_index_weights,
    payload_valve_weights,
    logistic_valve_addend,
    focus_exit_weights,
    focus_exit_addend,
):
    seq_count, res_count, feature_width = vertical_pieces.shape
    inner_channel_width = HEAD_COUNT * HEAD_CHANNELS
    normed = layer_norm(vertical_pieces, focus_normal_factor, focus_normal_addend).reshape(
        seq_count * res_count, feature_width
    )
    query_key = jnp.dot(normed, probe_index_weights, preferred_element_type=jnp.float32)
    value_gate = jnp.dot(normed, payload_valve_weights, preferred_element_type=jnp.float32)
    head_shape = (seq_count, res_count, HEAD_COUNT, HEAD_CHANNELS)
    query_rows_all = (
        (query_key[:, :inner_channel_width] * HEAD_CHANNELS ** (-0.5))
        .astype(jnp.bfloat16)
        .reshape(head_shape)
    )
    key_rows = query_key[:, inner_channel_width:].astype(jnp.bfloat16).reshape(head_shape)
    value_rows = value_gate[:, :inner_channel_width].astype(jnp.bfloat16).reshape(head_shape)
    gating = jax.nn.sigmoid(value_gate[:, inner_channel_width:] + logistic_valve_addend)
    scores = jnp.einsum(
        "srhd,trhd->rhst", query_rows_all, key_rows, preferred_element_type=jnp.float32
    )
    allowed = jnp.transpose(present_mask > 0)[:, None, None, :]
    scores = jnp.where(allowed, scores, MASKED)
    exponent = jnp.exp(scores - jnp.max(scores, axis=-1, keepdims=True))
    weights = (exponent / jnp.sum(exponent, axis=-1, keepdims=True)).astype(jnp.bfloat16)
    attended = jnp.einsum(
        "rhst,trhd->srhd", weights, value_rows, preferred_element_type=jnp.float32
    )
    gated_rows = (attended.reshape(seq_count * res_count, inner_channel_width) * gating).astype(
        jnp.bfloat16
    )
    update = (
        jnp.dot(gated_rows, focus_exit_weights, preferred_element_type=jnp.float32)
        + focus_exit_addend
    )
    return (
        vertical_pieces.astype(jnp.float32) + update.reshape(seq_count, res_count, feature_width)
    ).astype(jnp.bfloat16)


def project_pairs(
    revised_tensor,
    present_mask,
    product_mean_layer_stretch,
    product_mean_layer_shift,
    twin_map_matrix,
    twin_map_shift,
):
    seq_count, res_count, feature_width = revised_tensor.shape
    normed = layer_norm(
        revised_tensor, product_mean_layer_stretch, product_mean_layer_shift
    ).reshape(seq_count * res_count, feature_width)
    projected = (
        jnp.dot(normed, twin_map_matrix, preferred_element_type=jnp.float32) + twin_map_shift
    )
    projected = projected.reshape(seq_count, res_count, 2 * OUTER_CHANNELS) * present_mask[
        :, :, None
    ].astype(jnp.float32)
    projected = projected.astype(jnp.bfloat16)
    return (projected[:, :, :OUTER_CHANNELS], projected[:, :, OUTER_CHANNELS:])


def pair_tile(left_rows, right_cols, live_rows, live_cols, couple_map_matrix, couple_map_shift):
    row_count = left_rows.shape[1]
    col_count = right_cols.shape[1]
    outer_sum = jnp.einsum(
        "sic,sje->ijce", left_rows, right_cols, preferred_element_type=jnp.float32
    )
    counts = jnp.einsum("si,sj->ij", live_rows, live_cols, preferred_element_type=jnp.float32)
    mean_terms = (
        outer_sum.reshape(row_count, col_count, OUTER_CHANNELS * OUTER_CHANNELS)
        / jnp.maximum(counts, 1.0)[:, :, None]
    ).astype(jnp.bfloat16)
    result = jnp.dot(
        mean_terms.reshape(row_count * col_count, OUTER_CHANNELS * OUTER_CHANNELS),
        couple_map_matrix,
        preferred_element_type=jnp.float32,
    )
    result = result + couple_map_shift
    return result.astype(jnp.bfloat16).reshape(row_count, col_count, PAIR_DIM)


def tiled_pairs(left_rows, right_cols, live_rows, live_cols, couple_map_matrix, couple_map_shift):
    return pair_tile(
        left_rows, right_cols, live_rows, live_cols, couple_map_matrix, couple_map_shift
    )


def shards(
    homolog_stack_tensor,
    occupancy_indicator,
    chain_existence_flags,
    focus_normal_factor,
    focus_normal_addend,
    probe_index_weights,
    payload_valve_weights,
    logistic_valve_addend,
    focus_exit_weights,
    focus_exit_addend,
    product_mean_layer_stretch,
    product_mean_layer_shift,
    twin_map_matrix,
    twin_map_shift,
    couple_map_matrix,
    couple_map_shift,
):
    vertical_pieces = exchange_by_chip(
        homolog_stack_tensor, (("dap_0", "dap_1"), "dap_2"), (1, 0), 1, 0
    )
    seq_count, res_local, feature_width = vertical_pieces.shape
    position = lax.axis_index(DAP)
    present_integer = occupancy_indicator * chain_existence_flags[:, None]
    live_all = present_integer.astype(jnp.bfloat16)
    live_own = lax.dynamic_slice_in_dim(present_integer, position * res_local, res_local, 1)
    revised_tensor = heed_across_lanes(
        vertical_pieces,
        live_own,
        focus_normal_factor,
        focus_normal_addend,
        probe_index_weights,
        payload_valve_weights,
        logistic_valve_addend,
        focus_exit_weights,
        focus_exit_addend,
    )
    left_own, right_own = project_pairs(
        revised_tensor,
        live_own,
        product_mean_layer_stretch,
        product_mean_layer_shift,
        twin_map_matrix,
        twin_map_shift,
    )
    live_rows = live_own.astype(jnp.bfloat16)
    pair_rows = tiled_pairs(
        left_own,
        lax.all_gather(right_own, DAP, axis=1, tiled=True),
        live_rows,
        live_all,
        couple_map_matrix,
        couple_map_shift,
    )
    return (revised_tensor, pair_rows)


def solution(mesh):
    split = Mesh(
        mesh.devices.reshape(mesh.shape["grp"], 8, 8, 2), ("grp", "dap_0", "dap_1", "dap_2")
    )
    return jax.shard_map(
        shards,
        mesh=split,
        in_specs=(
            P(GRP_DAP, None, None),
            P("grp", None),
            P("grp"),
            P(),
            P(),
            P(),
            P(),
            P(),
            P(),
            P(),
            P(),
            P(),
            P(),
            P(),
            P(),
            P(),
        ),
        out_specs=(P("grp", DAP, None), P(GRP_DAP, None, None)),
        check_vma=False,
    )
```

profile of v0, /device:TPU:513, one launch (start us, length us, event | category | flops | bytes accessed | tf_op | source)
XLA Modules:
  0.0 220.7 jit_solution(6684543563587633720)
XLA Ops:
  7.2 1.2 reshape.120
  8.6 24.2 %all_to_all.10 = bf16[64,2,2,4,256]{4,3,2,0,1:T(4,128)(2,1)S(1)} all-to-all(bf16[64,2,2,4,256]{4,3,2,0,1:T(4,128)(2,1)S(1)} %copy.89), channel_id=1, replica_groups=mesh['grp'=2,'dap_0'=8,'dap_1'=8,'dap_2'=2] {'dap_2'}, dimensions={1} | all-to-all | bytes 1048576 | tf_op jit(solution)/shard_map/all_to_all | solution.py:35
  32.8 1.0 copy.90
  33.8 6.5 %all-to-all-start.1 = ((bf16[64,2,2,4,256]{4,3,2,1,0:T(4,128)(2,1)}), bf16[64,2,2,4,256]{4,3,2,1,0:T(4,128)(2,1)S(1)}, u32[]{:S(2)}, u32[]{:S(2)}) async-start(bf16[64,2,2,4,256]{4,3,2,1,0:T(4,128)(2,1)} %copy.90), calls=%async_computation.1 | async-start | bytes 1048576 | tf_op jit(solution)/shard_map/all_to_all | solution.py:35
  40.3 0.2 all-gather.2.cloned.1.call-start
  40.5 1.2 copy.98
  41.8 0.7 broadcast_multiply_fusion
  42.6 14.5 %all-to-all-done.1 = bf16[64,2,2,4,256]{4,3,2,1,0:T(4,128)(2,1)S(1)} async-done(((bf16[64,2,2,4,256]{4,3,2,1,0:T(4,128)(2,1)}), bf16[64,2,2,4,256]{4,3,2,1,0:T(4,128)(2,1)S(1)}, u32[]{:S(2)}, u32[]{:S(2)}) %all-to-all-start.1) | async-done | bytes 524320 | tf_op jit(solution)/shard_map/all_to_all | solution.py:35
  57.0 0.5 convert_reduce_fusion.1
  58.0 0.9 multiply_reduce_fusion
  59.4 0.5 fusion.47
  60.1 1.9 reshape.124
  62.1 1.9 reshape.123
  63.9 1.4 fusion.48
  65.4 1.3 copy-done.2
  66.8 1.9 reshape.122
  68.7 3.9 %fusion.16 = f32[4,8,256,256]{2,3,1,0:T(8,128)S(1)} fusion(bf16[256,4,8,32]{3,2,1,0:T(8,128)(2,1)} %reshape.124, bf16[256,4,8,32]{3,2,1,0:T(8,128)(2,1)} %reshape.123), kind=kOutput, calls=%fused_computation.16 | convolution fusion | flops 134217728 | bytes 9437184 | tf_op jit(solution)/shard_map/srhd,trhd->rhst/dot_general | solution.py:80
  72.5 2.4 %fusion.49 = (f32[4,8,256]{2,1,0:T(8,128)S(1)}, f32[4,8,256,256]{2,3,1,0:T(8,128)S(1)}) fusion(f32[4,8,256,256]{2,3,1,0:T(8,128)S(1)} %fusion.16, pred[4,256]{1,0:T(4,128)(4,1)S(1)} %compare_bitcast_fusion), kind=kOutput, calls=%fused_computation.69 | output fusion | flops 8388863 | bytes 16811008 | tf_op jit(solution)/shard_map/sub | solution.py:85
  74.9 1.4 fusion.19
  76.4 4.4 %copy.103 = f32[256,4,8,32]{3,2,1,0:T(8,128)} copy(f32[256,4,8,32]{0,3,2,1:T(8,128)S(1)} %fusion.19) | data formatting | bytes 2097152 | tf_op jit(solution)/shard_map/rhst,trhd->srhd/transpose | solution.py:87
  80.8 3.6 %reshape.125 = f32[1024,256]{1,0:T(8,128)S(1)} reshape(f32[256,4,8,32]{3,2,1,0:T(8,128)} %copy.103) | data formatting | bytes 2097152 | tf_op jit(solution)/shard_map/reshape | solution.py:90
  84.4 2.7 %convert_reduce_fusion = (f32[1024]{0:T(1024)S(1)}, bf16[1024,256]{1,0:T(8,128)(2,1)S(1)}, f32[1024,256]{1,0:T(8,128)}) fusion(f32[1024,256]{1,0:T(8,128)S(1)} %reshape.131, f32[256]{0:T(256)S(1)} %copy-done.9, bf16[256,256]{1,0:T(8,128)(2,1)S(1)} %copy-done.7, f32[1024,256]{1,0:T(8,128)S(1)} %reshape.125, f32[1024,512]{1,0:T(8,128)} %copy-done.2, ...), kind=kOutput, calls=%fused_computation.22 | convolution fusion | flops 137100288 | bytes 4855808 | tf_op jit(solution)/shard_map/dot_general | solution.py:94
  87.1 0.4 fusion.25
  87.6 0.5 convolution_add_fusion.1
  88.5 0.6 slice.30
  89.4 1.5 reshape.126
  90.9 1.1 fusion.35
  92.0 83.1 %all-gather.2.cloned.1.call-done = bf16[256,512,32]{0,2,1:T(8,128)(2,1)} async-done(((bf16[256,4,32]{0,2,1:T(8,128)(2,1)}), bf16[256,512,32]{0,2,1:T(8,128)(2,1)}) %all-gather.2.cloned.1.call-update) | async-done | bytes 8388624 | tf_op jit(solution)/shard_map/all_gather | solution.py:198
  175.1 16.3 %fusion.10 = f32[4,512,32,32]{1,2,0,3:T(8,128)} fusion(bf16[256,512,32,1]{0,2,1,3:T(8,128)(2,1)} %bitcast.35, bf16[256,4,64]{0,2,1:T(8,128)(2,1)S(1)} %multiply_convert_fusion), kind=kOutput, calls=%fused_computation.12 | convolution fusion | flops 1073741824 | bytes 16842752 | tf_op jit(solution)/shard_map/sic,sje->ijce/dot_general | solution.py:127
  191.4 12.2 %copy.107 = f32[4,512,32,32]{1,0,3,2:T(4,128)} copy(f32[4,512,32,32]{1,2,0,3:T(8,128)} %fusion.10) | data formatting | bytes 16777216 | tf_op jit(solution)/shard_map/sic,sje->ijce/transpose | solution.py:127
  203.7 7.5 %copy.117 = f32[128,8,4,512]{3,1,2,0:T(8,128)S(1)} copy(f32[128,8,4,512]{3,2,1,0:T(4,128)} %bitcast.34) | data formatting | bytes 16777216
  211.2 2.1 fusion.14
  (52 shorter events, 2.2 us)
Async XLA Ops:
  7.2 52.2 %copy-start = (bf16[256,512]{1,0:T(8,128)(2,1)S(1)}, bf16[256,512]{1,0:T(8,128)(2,1)}, u32[]{:S(2)}) copy-start(bf16[256,512]{1,0:T(8,128)(2,1)} %param.21) | copy-start | bytes 786436
  7.2 52.2 %copy-start.4 = (f32[256]{0:T(256)S(1)}, f32[256]{0:T(256)}, u32[]{:S(2)}) copy-start(f32[256]{0:T(256)} %param.20) | copy-start | bytes 3076
  7.2 52.2 %copy-start.5 = (f32[256]{0:T(256)S(1)}, f32[256]{0:T(256)}, u32[]{:S(2)}) copy-start(f32[256]{0:T(256)} %param.19) | copy-start | bytes 3076
  33.8 23.2 %all-to-all-start.1 = ((bf16[64,2,2,4,256]{4,3,2,1,0:T(4,128)(2,1)}), bf16[64,2,2,4,256]{4,3,2,1,0:T(4,128)(2,1)S(1)}, u32[]{:S(2)}, u32[]{:S(2)}) async-start(bf16[64,2,2,4,256]{4,3,2,1,0:T(4,128)(2,1)} %copy.90), calls=%async_computation.1 | async-start | bytes 1048576 | tf_op jit(solution)/shard_map/all_to_all | solution.py:35
  40.3 134.8 %all-gather.2.cloned.1.call-start = ((), (), s32[]{:S(2)}) async-start(), calls=%async_computation.2 | async-start | bytes 8454144 | tf_op jit(solution)/shard_map/all_gather | solution.py:198
  65.4 1.3 copy-start.2
  72.5 2.4 %copy-start.3 = (bf16[256,4,8,32]{3,2,1,0:T(8,128)(2,1)S(1)}, bf16[256,4,8,32]{3,2,1,0:T(8,128)(2,1)}, u32[]{:S(2)}) copy-start(bf16[256,4,8,32]{3,2,1,0:T(8,128)(2,1)} %reshape.122) | copy-start | bytes 1572868
  76.4 8.0 %copy-start.7 = (bf16[256,256]{1,0:T(8,128)(2,1)S(1)}, bf16[256,256]{1,0:T(8,128)(2,1)}, u32[]{:S(2)}) copy-start(bf16[256,256]{1,0:T(8,128)(2,1)} %param.24) | copy-start | bytes 393220
  76.4 8.0 %copy-start.9 = (f32[256]{0:T(256)S(1)}, f32[256]{0:T(256)}, u32[]{:S(2)}) copy-start(f32[256]{0:T(256)} %param.25) | copy-start | bytes 3076
  76.4 8.0 %copy-start.10 = (f32[256]{0:T(256)S(1)}, f32[256]{0:T(256)}, u32[]{:S(2)}) copy-start(f32[256]{0:T(256)} %param.23) | copy-start | bytes 3076
  76.4 11.1 %copy-start.8 = (bf16[256,64]{0,1:T(8,128)(2,1)S(1)}, bf16[256,64]{0,1:T(8,128)(2,1)}, u32[]{:S(2)}) copy-start(bf16[256,64]{0,1:T(8,128)(2,1)} %param.28) | copy-start | bytes 98308
  76.4 11.1 %copy-start.11 = (f32[256]{0:T(256)S(1)}, f32[256]{0:T(256)}, u32[]{:S(2)}) copy-start(f32[256]{0:T(256)} %param.27) | copy-start | bytes 3076
  76.4 11.1 %copy-start.12 = (f32[256]{0:T(256)S(1)}, f32[256]{0:T(256)}, u32[]{:S(2)}) copy-start(f32[256]{0:T(256)} %param.26) | copy-start | bytes 3076
  76.4 11.1 %copy-start.13 = (f32[64]{0:T(128)S(1)}, f32[64]{0:T(128)}, u32[]{:S(2)}) copy-start(f32[64]{0:T(128)} %param.29) | copy-start | bytes 772
  203.7 7.5 %copy-start.6 = (bf16[1024,128]{1,0:T(8,128)(2,1)S(1)}, bf16[1024,128]{1,0:T(8,128)(2,1)}, u32[]{:S(2)}) copy-start(bf16[1024,128]{1,0:T(8,128)(2,1)} %param.30) | copy-start | bytes 786436
  203.7 7.5 %copy-start.14 = (f32[128]{0:T(128)S(1)}, f32[128]{0:T(128)}, u32[]{:S(2)}) copy-start(f32[128]{0:T(128)} %param.31) | copy-start | bytes 1540
  211.2 2.1 copy-start.1
Sparse Core Ops, SparseCore 0:
  89.3 85.7 all-gather.1
where the time goes:
time: 224 us; the launch traced here: 221 us
  waiting for transfers between devices  97.6 us (44%)
  local copies, waits for them, and re-layouts  42.1 us (19%)
  matrix products  29.1 us (13%)
  blocking collectives  24.2 us (11%)
  between operations  14.9 us (7%)
  starting transfers between devices  6.73 us (3%)
  other arithmetic  6.07 us (3%)
    all_gather x1, waiting for transfers between devices, shards(): lax.all_gather(right_own, DAP, axis=1, tiled=True)  83.1 us
    all_to_all x1, blocking collectives, exchange_in_order(): lax.all_to_all(parts, axes[k], split_axis=k, concat_axis=k, tiled=True)  24.2 us
    dot_general x1, matrix products, pair_tile(): jnp.einsum('sic,sje->ijce', left_rows, right_cols, preferred_element_type...  16.3 us
    all_to_all x1, waiting for transfers between devices, exchange_in_order(): lax.all_to_all(parts, axes[k], split_axis=k, concat_axis=k, tiled=True)  14.5 us
    transpose x1, local copies, waits for them, and re-layouts, pair_tile(): jnp.einsum('sic,sje->ijce', left_rows, right_cols, preferred_element_type...  12.2 us
    unnamed x33, local copies, waits for them, and re-layouts  10.2 us
    all_to_all x1, starting transfers between devices, exchange_in_order(): lax.all_to_all(parts, axes[k], split_axis=k, concat_axis=k, tiled=True)  6.49 us
  transfers between devices with their start and end apart: 2, of which 2 were waited for; matrix products, arithmetic and copies ran while one was open for 2% of the time, Pallas kernels for 0%

commit v1 on v0

v1 whole, which is shorter than its diff:
```python
import functools

import jax
import jax.numpy as jnp
from jax import lax
from jax.experimental import pallas as pl
from jax.experimental.pallas import tpu as pltpu
from jax.sharding import Mesh
from jax.sharding import PartitionSpec as P

HEAD_COUNT = 8
HEAD_CHANNELS = 32
OUTER_CHANNELS = 32
PAIR_DIM = 128
DAP = ("dap_0", "dap_1", "dap_2")
GRP_DAP = ("grp", "dap_0", "dap_1", "dap_2")
F32 = jnp.float32
BF16 = jnp.bfloat16
VMEM_LIMIT = 60 * 1024 * 1024


EPSILON = 1e-05
MASKED = -100000.0


def in_blocks(value, dim, count):
    shape = value.shape
    parts = value.reshape(*shape[:dim], count, shape[dim] // count, *shape[dim + 1 :])
    return jnp.moveaxis(parts, dim, 0)


def joined_along(parts, dim):
    parts = jnp.moveaxis(parts, 0, dim)
    shape = parts.shape
    return parts.reshape(*shape[:dim], shape[dim] * shape[dim + 1], *shape[dim + 2 :])


def exchange_in_order(parts, axes, turns):
    shape = [lax.axis_size(a) for a in axes]
    parts = parts.reshape(*shape, *parts.shape[1:])
    for k in turns:
        parts = lax.all_to_all(parts, axes[k], split_axis=k, concat_axis=k, tiled=True)
    return parts.reshape(-1, *parts.shape[len(axes) :])


def exchange_by_chip(value, groups, turns, split_dim, concat_dim):
    count = lax.axis_size(groups[0]) * lax.axis_size(groups[1])
    parts = in_blocks(value, split_dim, count)
    return joined_along(exchange_in_order(parts, groups, turns), concat_dim)


def normalize(widened, gain, offset):
    centred = widened - jnp.mean(widened, axis=-1, keepdims=True)
    variance = jnp.mean(centred * centred, axis=-1, keepdims=True)
    return (centred * lax.rsqrt(variance + EPSILON) * gain + offset).astype(BF16)


def contract_lanes(a, b):
    return lax.dot_general(a, b, (((1,), (1,)), ((), ())), preferred_element_type=F32)


def attend_kernel(
    x_ref, keep_ref, gain_ref, offset_ref, qk_ref, vg_ref, gate_ref, exit_ref, exit_add_ref,
    gain2_ref, offset2_ref, twin_l_ref, twin_r_ref, shift_l_ref, shift_r_ref, live_l_ref,
    live_r_ref, after_ref, left_ref, right_ref, left_sum, right_sum,
):
    sites, seqs, width = x_ref.shape
    inner = HEAD_COUNT * HEAD_CHANNELS
    head_of_lane = lax.broadcasted_iota(jnp.int32, (1, inner), 1) // HEAD_CHANNELS
    left_sum[...] = jnp.zeros_like(left_sum)
    right_sum[...] = jnp.zeros_like(right_sum)

    def one_site(r, carry):
        x = x_ref[r].astype(F32)
        normed = normalize(x, gain_ref[...], offset_ref[...])
        query_key = jnp.dot(normed, qk_ref[...], preferred_element_type=F32)
        value_gate = jnp.dot(normed, vg_ref[...], preferred_element_type=F32)
        query = (query_key[:, :inner] * HEAD_CHANNELS ** (-0.5)).astype(BF16)
        key = query_key[:, inner:].astype(BF16)
        value = value_gate[:, :inner].astype(BF16)
        gate = jax.nn.sigmoid(value_gate[:, inner:] + gate_ref[...])
        keep = keep_ref[r] > 0
        mixed = jnp.zeros((seqs, inner), F32)
        for h in range(HEAD_COUNT):
            own = head_of_lane == h
            query_h = query * own.astype(F32).astype(BF16)
            scores = jnp.where(keep, contract_lanes(query_h, key), MASKED)
            exponent = jnp.exp(scores - jnp.max(scores, axis=-1, keepdims=True))
            total = jnp.sum(exponent, axis=-1, keepdims=True)
            part = jnp.dot(exponent.astype(BF16), value, preferred_element_type=F32)
            mixed = jnp.where(own, part * (1.0 / total), mixed)
        gated = (mixed * gate).astype(BF16)
        update = jnp.dot(gated, exit_ref[...], preferred_element_type=F32) + exit_add_ref[...]
        after = (x + update).astype(BF16)
        after_ref[r] = after
        again = normalize(after.astype(F32), gain2_ref[...], offset2_ref[...])
        site_of_lane = (
            lax.broadcasted_iota(jnp.int32, (1, sites * OUTER_CHANNELS), 1) // OUTER_CHANNELS
        )
        site_of_row = lax.broadcasted_iota(jnp.int32, (sites * OUTER_CHANNELS, 1), 0) % sites
        twin_l = twin_l_ref[...] * (site_of_lane == r).astype(F32).astype(BF16)
        twin_r = twin_r_ref[...] * (site_of_row == r).astype(F32).astype(BF16)
        left_sum[...] += jnp.dot(again, twin_l, preferred_element_type=F32)
        right_sum[...] += contract_lanes(twin_r, again)
        return carry

    lax.fori_loop(0, sites, one_site, 0)
    left_ref[...] = ((left_sum[...] + shift_l_ref[...]) * live_l_ref[...]).astype(BF16)
    right_ref[...] = ((right_sum[...] + shift_r_ref[...]) * live_r_ref[...]).astype(BF16)


def attend(x, keep, *rest):
    sites, seqs, width = x.shape
    pack = sites * OUTER_CHANNELS
    return pl.pallas_call(
        attend_kernel,
        out_shape=(
            jax.ShapeDtypeStruct(x.shape, BF16),
            jax.ShapeDtypeStruct((seqs, pack), BF16),
            jax.ShapeDtypeStruct((pack, seqs), BF16),
        ),
        scratch_shapes=[pltpu.VMEM((seqs, pack), F32), pltpu.VMEM((pack, seqs), F32)],
        compiler_params=pltpu.CompilerParams(vmem_limit_bytes=VMEM_LIMIT),
        name="attend",
    )(x, keep, *rest)


def pair_kernel(
    right_ref, left_ref, live_t_ref, live_l_ref, couple_ref, shift_ref, out_ref,
    inverse, terms, blocks,
):
    step = pl.program_id(0)
    owners, pack, seqs = right_ref.shape
    sites = out_ref.shape[0]
    chip_rows = 2 * sites
    halves = OUTER_CHANNELS // 2

    @pl.when(step == 0)
    def _():
        counts = jnp.dot(live_t_ref[...], live_l_ref[...], preferred_element_type=F32)
        inverse[...] = 1.0 / jnp.maximum(counts, 1.0)
        blocks[...] = jnp.zeros_like(blocks)
        for e in range(OUTER_CHANNELS):
            for i in range(sites):
                row = (e % 2) * pack + i * OUTER_CHANNELS
                blocks[e // 2, row : row + OUTER_CHANNELS, i * PAIR_DIM : (i + 1) * PAIR_DIM] = (
                    couple_ref[e]
                )

    lower = lax.broadcasted_iota(jnp.int32, (1, chip_rows, 1), 1) < sites
    left = left_ref[...]

    def four(u, carry):
        quad = right_ref[pl.ds(4 * u, 4)].reshape(4 * pack, seqs)
        sums = jnp.dot(quad, left, preferred_element_type=F32)
        sums = sums.reshape(4, halves, chip_rows, pack)
        even, odd = [], []
        for t in range(2):
            a, b = sums[2 * t], sums[2 * t + 1]
            first = pl.multiple_of((step * owners + 4 * u + 2 * t) * sites, chip_rows)
            scale = inverse[pl.ds(first, chip_rows), :][None]
            even.append(jnp.where(lower, a, pltpu.roll(b, sites, 1)) * scale)
            odd.append(jnp.where(lower, pltpu.roll(a, sites, 1), b) * scale)
        rows = pl.ds(pl.multiple_of((step * owners + 4 * u) * sites, 2 * chip_rows), 2 * chip_rows)
        terms[:, rows, :pack] = jnp.concatenate(even, axis=1).astype(BF16)
        terms[:, rows, pack:] = jnp.concatenate(odd, axis=1).astype(BF16)
        return carry

    lax.fori_loop(0, owners // 4, four, 0)

    @pl.when(step == pl.num_programs(0) - 1)
    def _():
        total = jnp.dot(terms[0], blocks[0], preferred_element_type=F32)
        for e in range(1, halves):
            total = total + jnp.dot(terms[e], blocks[e], preferred_element_type=F32)
        for i in range(sites):
            part = total[:, i * PAIR_DIM : (i + 1) * PAIR_DIM] + shift_ref[...]
            out_ref[i] = part.astype(BF16)


def pairs(right_all, left, live_t, live_l, couple, shift):
    owners, pack, seqs = right_all.shape
    residues = live_t.shape[0]
    sites = pack // OUTER_CHANNELS
    steps = 4
    whole = lambda *shape: pl.BlockSpec(shape, lambda g: (0,) * len(shape))
    return pl.pallas_call(
        pair_kernel,
        grid=(steps,),
        in_specs=[
            pl.BlockSpec((owners // steps, pack, seqs), lambda g: (g, 0, 0)),
            whole(*left.shape),
            whole(*live_t.shape),
            whole(*live_l.shape),
            whole(*couple.shape),
            whole(*shift.shape),
        ],
        out_specs=whole(sites, residues, PAIR_DIM),
        out_shape=jax.ShapeDtypeStruct((sites, residues, PAIR_DIM), BF16),
        scratch_shapes=[
            pltpu.VMEM((residues, pack), F32),
            pltpu.VMEM((OUTER_CHANNELS // 2, residues, 2 * pack), BF16),
            pltpu.VMEM((OUTER_CHANNELS // 2, 2 * pack, sites * PAIR_DIM), BF16),
        ],
        compiler_params=pltpu.CompilerParams(
            vmem_limit_bytes=VMEM_LIMIT, dimension_semantics=("arbitrary",)
        ),
        name="pairs",
    )(right_all, left, live_t, live_l, couple, shift)


GATHER_RING = pltpu.CompilerParams(
    vmem_limit_bytes=VMEM_LIMIT, collective_id=1, has_side_effects=True
)


def ring_order(size):
    far = size // 2
    offsets = [0]
    for hop in range(1, far):
        offsets += [-hop, hop]
    offsets.append(far)
    events = []
    for hop in range(1, far + 1):
        events.append((3.0 * hop, 0, hop, 0))
    for offset in offsets:
        ready = 3.0 * abs(offset)
        for hop in range(1, far + 1):
            events.append((ready + 2.7 * hop + 0.01, 1, hop, offset))
    return sorted(events, key=lambda event: event[:2]), offsets


def gather_kernel(size, own_ref, all_ref, held, p_recv, s_recv, x_recv, send_sem, out_sem, in_sem):
    far = size // 2
    y, x, core = (lax.axis_index(a) for a in DAP)
    half = own_ref.shape[0] // 2

    def at(first, second):
        row = jnp.where(core == 0, second, first)
        column = jnp.where(core == 0, first, second)
        return lax.rem(row + size, size), lax.rem(column + size, size)

    main = jnp.where(core == 0, x, y)
    side = jnp.where(core == 0, y, x)

    def device(first, second):
        row, column = at(first, second)
        return {"dap_0": row, "dap_1": column}

    def slot(first, second, which):
        row, column = at(first, second)
        return (row * size + column) * 2 + which

    partner = {"dap_2": 1 - core}
    neighbours = [
        device(main + 1, side), device(main - 1, side), device(main, side + 1),
        device(main, side - 1), partner,
    ]
    barrier = pltpu.get_barrier_semaphore()
    own_copy = pltpu.make_async_copy(own_ref, held.at[slot(main, side, core)], in_sem)
    own_copy.start()
    for neighbour in neighbours:
        pl.semaphore_signal(
            barrier, inc=1, device_id=neighbour, device_id_type=pl.DeviceIdType.MESH
        )
    pl.semaphore_wait(barrier, len(neighbours))
    own_copy.wait()

    def piece(first, second, which, hop, sign):
        ref = held.at[slot(first, second, which)]
        if hop < far:
            return ref
        return ref.at[pl.ds(0 if sign > 0 else half, half)]

    def remote(ref, recv, target):
        return pltpu.make_async_remote_copy(
            src_ref=ref, dst_ref=ref, send_sem=send_sem, recv_sem=recv,
            device_id=target, device_id_type=pl.DeviceIdType.MESH,
        )

    def along_main(hop, sign):
        ref = piece(main - sign * (hop - 1), side, core, hop, sign)
        remote(ref, p_recv.at[(sign + 1) // 2, hop - 1], device(main + sign, side)).start()

    def along_side(offset, index, hop, sign):
        ref = piece(main + offset, side - sign * (hop - 1), core, hop, sign)
        remote(ref, s_recv.at[index, (sign + 1) // 2, hop - 1], device(main, side + sign)).start()

    def finished(first, second, order):
        ref = held.at[slot(first, second, core)]
        remote(ref, x_recv.at[order], partner).start()
        pltpu.make_async_copy(ref, all_ref.at[slot(first, second, core)], out_sem).start()
        done.append((first, second))

    def from_partner(order):
        first, second = done[order]
        ref = held.at[swapped_slot(first, second)]
        remote(ref, x_recv.at[order], partner).wait_recv()
        pltpu.make_async_copy(ref, all_ref.at[swapped_slot(first, second)], out_sem).start()

    def swapped_slot(first, second):
        d_first, d_second = first - main, second - side
        row = jnp.where(core == 0, main_row + d_first, main_row + d_second)
        column = jnp.where(core == 0, main_column + d_second, main_column + d_first)
        row, column = lax.rem(row + size, size), lax.rem(column + size, size)
        return (row * size + column) * 2 + (1 - core)

    main_row, main_column = y, x
    done = []
    events, offsets = ring_order(size)
    for sign in (1, -1):
        along_main(1, sign)
        along_side(0, 0, 1, sign)
    finished(main, side, 0)
    lag, taken = 6, 0
    for _, kind, hop, offset in events:
        if kind == 0:
            for sign in (1, -1):
                ref = piece(main - sign * hop, side, core, hop, sign)
                remote(ref, p_recv.at[(sign + 1) // 2, hop - 1], partner).wait_recv()
                if hop < far:
                    along_main(hop + 1, sign)
                    index = offsets.index(-sign * hop)
                    for way in (1, -1):
                        along_side(-sign * hop, index, 1, way)
                    finished(main - sign * hop, side, len(done))
            if hop == far:
                for way in (1, -1):
                    along_side(far, offsets.index(far), 1, way)
                finished(main + far, side, len(done))
        else:
            index = offsets.index(offset)
            for sign in (1, -1):
                ref = piece(main + offset, side - sign * hop, core, hop, sign)
                remote(ref, s_recv.at[index, (sign + 1) // 2, hop - 1], partner).wait_recv()
                if hop < far:
                    along_side(offset, index, hop + 1, sign)
                    finished(main + offset, side - sign * hop, len(done))
            if hop == far:
                finished(main + offset, side + far, len(done))
        while taken < len(done) - lag:
            from_partner(taken)
            taken += 1
    while taken < len(done):
        from_partner(taken)
        taken += 1
    sent = (size - 1) * (size + 1) + size * size
    drained = held.at[pl.ds(0, sent)]
    pltpu.make_async_copy(drained, drained, send_sem).wait()
    pltpu.make_async_copy(held, all_ref, out_sem).wait()


def gather_right(own, size):
    owners = 2 * size * size
    return pl.pallas_call(
        functools.partial(gather_kernel, size),
        out_shape=jax.ShapeDtypeStruct((owners, *own.shape), own.dtype),
        in_specs=[pl.BlockSpec(memory_space=pl.ANY)],
        out_specs=pl.BlockSpec(memory_space=pl.ANY),
        scratch_shapes=[
            pltpu.VMEM((owners, *own.shape), own.dtype),
            pltpu.SemaphoreType.DMA((2, size // 2)),
            pltpu.SemaphoreType.DMA((size, 2, size // 2)),
            pltpu.SemaphoreType.DMA((size * size,)),
            pltpu.SemaphoreType.DMA,
            pltpu.SemaphoreType.DMA,
            pltpu.SemaphoreType.DMA,
        ],
        compiler_params=GATHER_RING,
        name="gather_right",
    )(own)


def shards(
    homolog_stack_tensor,
    occupancy_indicator,
    chain_existence_flags,
    focus_normal_factor,
    focus_normal_addend,
    probe_index_weights,
    payload_valve_weights,
    logistic_valve_addend,
    focus_exit_weights,
    focus_exit_addend,
    product_mean_layer_stretch,
    product_mean_layer_shift,
    twin_map_matrix,
    twin_map_shift,
    couple_map_matrix,
    couple_map_shift,
):
    vertical_pieces = exchange_by_chip(
        homolog_stack_tensor, (("dap_0", "dap_1"), "dap_2"), (1, 0), 1, 0
    )
    seq_count, res_local, feature_width = vertical_pieces.shape
    position = lax.axis_index(DAP)
    present = occupancy_indicator * chain_existence_flags[:, None]
    live_own = lax.dynamic_slice_in_dim(present, position * res_local, res_local, 1)
    live_t = present.T.astype(BF16)
    own_t = live_own.T.astype(F32)
    live_l = jnp.repeat(live_own, OUTER_CHANNELS, axis=1)
    live_r = jnp.tile(own_t, (OUTER_CHANNELS, 1))
    row = lambda v: v[None, :]
    after, left, right = attend(
        jnp.transpose(vertical_pieces, (1, 0, 2)),
        own_t[:, None, :],
        row(focus_normal_factor),
        row(focus_normal_addend),
        probe_index_weights,
        payload_valve_weights,
        row(logistic_valve_addend),
        focus_exit_weights,
        row(focus_exit_addend),
        row(product_mean_layer_stretch),
        row(product_mean_layer_shift),
        jnp.tile(twin_map_matrix[:, :OUTER_CHANNELS], (1, res_local)),
        jnp.repeat(twin_map_matrix[:, OUTER_CHANNELS:].T, res_local, axis=0),
        row(jnp.tile(twin_map_shift[:OUTER_CHANNELS], res_local)),
        jnp.repeat(twin_map_shift[OUTER_CHANNELS:], res_local)[:, None],
        live_l.astype(F32),
        live_r,
    )
    right_all = gather_right(right, lax.axis_size("dap_0"))
    couple = jnp.transpose(
        couple_map_matrix.reshape(OUTER_CHANNELS, OUTER_CHANNELS, PAIR_DIM), (1, 0, 2)
    )
    pair_rows = pairs(
        right_all, left, live_t, live_l.astype(BF16), couple, row(couple_map_shift)
    )
    return (jnp.transpose(after, (1, 0, 2)), pair_rows)


def solution(mesh):
    split = Mesh(
        mesh.devices.reshape(mesh.shape["grp"], 8, 8, 2), ("grp", "dap_0", "dap_1", "dap_2")
    )
    return jax.shard_map(
        shards,
        mesh=split,
        in_specs=(
            P(GRP_DAP, None, None),
            P("grp", None),
            P("grp"),
            P(),
            P(),
            P(),
            P(),
            P(),
            P(),
            P(),
            P(),
            P(),
            P(),
            P(),
            P(),
            P(),
        ),
        out_specs=(P("grp", DAP, None), P(GRP_DAP, None, None)),
        check_vma=False,
    )
```

time: 224 us -> 117 us (0.52); the launches traced: 221 us -> 117 us
  waiting for transfers between devices: 97.6 us -> 5.04 us
  Pallas kernels: 0 us -> 62.2 us
  matrix products: 29.1 us -> 0 us
  local copies, waits for them, and re-layouts: 42.1 us -> 16.6 us
  between operations: 14.9 us -> 0.7 us
  other arithmetic: 6.07 us -> 1.47 us
    all_gather x1 -> x0, waiting for transfers between devices: 83.1 us -> none  [shards(): lax.all_gather(right_own, DAP, axis=1, tiled=True)]
    pallas_call x0 -> x3, Pallas kernels: none -> 62.2 us  [the longest x1 40.1 us: gather_right(): pl.pallas_call(functools.partial(gather_kernel, size), out_shape=jax.Shap...]
    dot_general x9 -> x0, matrix products: 29.1 us -> none  [the longest x1 16.3 us: pair_tile(): jnp.einsum('sic,sje->ijce', left_rows, right_cols, preferred_element_type...]
    transpose x2 -> x1, local copies, waits for them, and re-layouts: 16.6 us -> 0.74 us  [shards(): twin_map_matrix[:, OUTER_CHANNELS:]]
    all_to_all x1, waiting for transfers between devices: 14.5 us -> 5.04 us  [exchange_in_order(): lax.all_to_all(parts, axes[k], split_axis=k, concat_axis=k, tiled=True)]
    reshape x6 -> x2, local copies, waits for them, and re-layouts: 11 us -> 2.42 us  [the longest x1 1.77 us: shards(): couple_map_matrix.reshape(OUTER_CHANNELS, OUTER_CHANNELS, PAIR_DIM)]
    unnamed x33 -> x2, local copies, waits for them, and re-layouts: 10.2 us -> 3.48 us
    another operation x0 -> x8, local copies, waits for them, and re-layouts: none -> 3.79 us  [the longest x1 0.99 us: joined_along(): parts.reshape(*shape[:dim], shape[dim] * shape[dim + 1], *shape[dim + 2:])]
  transfers between devices with their start and end apart: 2 -> 1, of which waited for: 2 -> 1; matrix products, arithmetic and copies ran while one was open for 2% -> 10% of each run, Pallas kernels for 0% -> 0%
where the time goes in v1:
time: 117 us
  Pallas kernels  62.2 us (53%)
  blocking collectives  24.2 us (21%)
  local copies, waits for them, and re-layouts  16.6 us (14%)
  starting transfers between devices  6.49 us (6%)
  waiting for transfers between devices  5.04 us (4%)
  other arithmetic  1.47 us (1%)
    pallas_call x1, Pallas kernels, gather_right(): pl.pallas_call(functools.partial(gather_kernel, size), out_shape=jax.Shap...  40.1 us
    all_to_all x1, blocking collectives, exchange_in_order(): lax.all_to_all(parts, axes[k], split_axis=k, concat_axis=k, tiled=True)  24.2 us
    pallas_call x1, Pallas kernels, pairs(): pl.pallas_call(pair_kernel, grid=(steps,), in_specs=[pl.BlockSpec((owners...  12.8 us
    pallas_call x1, Pallas kernels, attend(): pl.pallas_call(attend_kernel, out_shape=(jax.ShapeDtypeStruct(x.shape, BF...  9.32 us
    all_to_all x1, starting transfers between devices, exchange_in_order(): lax.all_to_all(parts, axes[k], split_axis=k, concat_axis=k, tiled=True)  6.49 us
    all_to_all x1, waiting for transfers between devices, exchange_in_order(): lax.all_to_all(parts, axes[k], split_axis=k, concat_axis=k, tiled=True)  5.04 us
    unnamed x2, local copies, waits for them, and re-layouts  3.48 us
  transfers between devices with their start and end apart: 1, of which 1 were waited for; matrix products, arithmetic and copies ran while one was open for 10% of the time, Pallas kernels for 0%

profile of v1, /device:TPU:513, one launch (start us, length us, event | category | flops | bytes accessed | tf_op | source)
XLA Modules:
  0.0 116.7 jit_solution(10148059956668792064)
XLA Ops:
  0.6 1.2 reshape.29
  1.8 0.5 copy.46
  2.3 24.2 %all_to_all.10 = bf16[64,2,2,4,256]{4,2,0,3,1:T(2,128)(2,1)S(1)} all-to-all(bf16[64,2,2,4,256]{4,2,0,3,1:T(2,128)(2,1)S(1)} %copy.46), channel_id=1, replica_groups=mesh['grp'=2,'dap_0'=8,'dap_1'=8,'dap_2'=2] {'dap_2'}, dimensions={1} | all-to-all | bytes 1048576 | tf_op jit(solution)/shard_map/all_to_all | solution.py:42
  26.6 1.2 copy.47
  27.7 6.5 %all-to-all-start.1 = ((bf16[64,2,2,4,256]{4,2,1,3,0:T(2,128)(2,1)}), bf16[64,2,2,4,256]{4,2,1,3,0:T(2,128)(2,1)S(1)}, u32[]{:S(2)}, u32[]{:S(2)}) async-start(bf16[64,2,2,4,256]{4,2,1,3,0:T(2,128)(2,1)} %copy.47), calls=%async_computation.1 | async-start | bytes 1048576 | tf_op jit(solution)/shard_map/all_to_all | solution.py:42
  34.2 0.8 fusion
  35.0 0.7 broadcast_in_dim_tile.3.shift_l_ref
  35.7 0.7 slice_bitcast_fusion
  36.4 0.7 reshape.31.twin_r_ref
  37.1 0.1 broadcast_in_dim.44
  37.2 0.7 broadcast_in_dim_reshape.4.shift_r_ref
  37.9 0.7 copy.51.twin_l_ref
  38.6 1.8 %copy.59 = bf16[32,32,128]{2,0,1:T(8,128)(2,1)} copy(bf16[32,32,128]{2,1,0:T(8,128)(2,1)} %bitcast.34) | data formatting | bytes 524288 | tf_op jit(solution)/shard_map/reshape | solution.py:425
  40.4 1.2 %copy.49 = s32[256,512]{0,1:T(8,128)S(1)} copy(s32[256,512]{1,0:T(8,128)} %param.17) | data formatting | bytes 1048576 | tf_op args[1]
  41.6 1.5 %convert_bitcast_fusion = (bf16[512,256]{1,0:T(8,128)(2,1)}, s32[256,512]{0,1:T(8,128)S(1)}) fusion(s32[256,512]{0,1:T(8,128)S(1)} %copy.49, s32[256]{0:T(256)} %param.18), kind=kLoop, calls=%fused_computation.1 | loop fusion | flops 262144 | bytes 1311744 | tf_op jit(solution)/shard_map/convert_element_type | solution.py:399
  43.1 0.6 copy.50.keep_ref
  43.7 0.7 copy.55.live_l_ref
  44.4 0.7 tile.28.live_r_ref
  45.1 0.8 copy.53.live_l_ref
  45.9 5.0 %all-to-all-done.1 = bf16[64,2,2,4,256]{4,2,1,3,0:T(2,128)(2,1)S(1)} async-done(((bf16[64,2,2,4,256]{4,2,1,3,0:T(2,128)(2,1)}), bf16[64,2,2,4,256]{4,2,1,3,0:T(2,128)(2,1)S(1)}, u32[]{:S(2)}, u32[]{:S(2)}) %all-to-all-start.1) | async-done | bytes 524320 | tf_op jit(solution)/shard_map/all_to_all | solution.py:42
  50.9 0.4 copy.48
  51.3 1.0 reshape_reshape.3
  52.3 9.3 %attend.1 = (bf16[4,256,256]{2,1,0:T(8,128)(2,1)}, bf16[256,128]{1,0:T(8,128)(2,1)}, bf16[128,256]{1,0:T(8,128)(2,1)}) custom-call(bf16[4,256,256]{2,1,0:T(8,128)(2,1)} %bitcast.28, f32[4,1,256]{2,1,0:T(1,128)} %copy.50.keep_ref, f32[1,256]{1,0:T(1,128)} %bitcast.38, f32[1,256]{1,0:T(1,128)} %bitcast.39, bf16[256,512]{1,0:T(8,128)(2,1)} %qk_ref.1, ...), custom_call_target="tpu_custom_call" | custom-call | tf_op jit(solution)/shard_map/attend/pallas_call | solution.py:115
  61.6 2.2 %copy.56 = bf16[256,4,256]{2,1,0:T(4,128)(2,1)} copy(bf16[256,4,256]{2,0,1:T(8,128)(2,1)} %bitcast.31) | data formatting | bytes 1048576
  63.9 40.1 %gather_right.1.right_ref = bf16[128,128,256]{2,1,0:T(8,128)(2,1)} custom-call(bf16[128,256]{1,0:T(8,128)(2,1)} %get-tuple-element.6.own_ref), custom_call_target="tpu_custom_call" | custom-call | tf_op jit(solution)/shard_map/gather_right/pallas_call | solution.py:355
  104.0 12.8 %pairs.1 = bf16[4,512,128]{2,1,0:T(8,128)(2,1)} custom-call(bf16[128,128,256]{2,1,0:T(8,128)(2,1)} %gather_right.1.right_ref, bf16[256,128]{1,0:T(8,128)(2,1)} %get-tuple-element.7.left_ref, bf16[512,256]{1,0:T(8,128)(2,1)} %get-tuple-element.16.live_t_ref, bf16[256,128]{1,0:T(8,128)(2,1)} %copy.55.live_l_ref, bf16[32,32,128]{2,1,0:T(8,128)(2,1)} %bitcast.30, ...), custom_call_target="tpu_custom_call" | custom-call | tf_op jit(solution)/shard_map/pairs/pallas_call | solution.py:187
  (7 shorter events, 0.1 us)
Async XLA Ops:
  27.7 23.2 %all-to-all-start.1 = ((bf16[64,2,2,4,256]{4,2,1,3,0:T(2,128)(2,1)}), bf16[64,2,2,4,256]{4,2,1,3,0:T(2,128)(2,1)S(1)}, u32[]{:S(2)}, u32[]{:S(2)}) async-start(bf16[64,2,2,4,256]{4,2,1,3,0:T(2,128)(2,1)} %copy.47), calls=%async_computation.1 | async-start | bytes 1048576 | tf_op jit(solution)/shard_map/all_to_all | solution.py:42

commit v2 on v1

v2 whole, which is shorter than its diff:
```python
import functools

import jax
import jax.numpy as jnp
from jax import lax
from jax.experimental import pallas as pl
from jax.experimental.pallas import tpu as pltpu
from jax.sharding import Mesh
from jax.sharding import PartitionSpec as P

HEAD_COUNT = 8
HEAD_CHANNELS = 32
OUTER_CHANNELS = 32
PAIR_DIM = 128
DAP = ("dap_0", "dap_1", "dap_2")
GRP_DAP = ("grp", "dap_0", "dap_1", "dap_2")
F32 = jnp.float32
BF16 = jnp.bfloat16
VMEM_LIMIT = 60 * 1024 * 1024


EPSILON = 1e-05
MASKED = -100000.0


def normalize(widened, gain, offset):
    centred = widened - jnp.mean(widened, axis=-1, keepdims=True)
    variance = jnp.mean(centred * centred, axis=-1, keepdims=True)
    return (centred * lax.rsqrt(variance + EPSILON) * gain + offset).astype(BF16)


def contract_lanes(a, b):
    return lax.dot_general(a, b, (((1,), (1,)), ((), ())), preferred_element_type=F32)


def one_hot(rows, columns, test):
    row = lax.broadcasted_iota(jnp.int32, (rows, columns), 0)
    column = lax.broadcasted_iota(jnp.int32, (rows, columns), 1)
    return jnp.where(test(row, column), 1.0, 0.0)


def attend_kernel(
    place_ref, x_ref, present_ref, chain_ref, gain_ref, offset_ref, qk_ref, vg_ref, gate_ref,
    exit_ref, exit_add_ref, gain2_ref, offset2_ref, twin_ref, shift_ref,
    after_ref, left_ref, right_ref, inverse_ref,
    xs, ys, keep, left_sum, right_sum,
):
    sites, seqs, width = xs.shape
    residues = present_ref.shape[1]
    pack = sites * OUTER_CHANNELS
    inner = HEAD_COUNT * HEAD_CHANNELS
    place = place_ref[0]
    core = lax.rem(place, 2)
    blocks = x_ref.shape[0] // (2 * sites * OUTER_CHANNELS)
    span = seqs // blocks

    pick = one_hot(
        sites * span, 2 * sites * span,
        lambda o, k: k == (o % span) * (2 * sites) + core * sites + o // span,
    ).astype(BF16)
    for b in range(blocks):
        rows = jnp.dot(
            pick, x_ref[2 * sites * span * b : 2 * sites * span * (b + 1), :],
            preferred_element_type=F32,
        ).astype(BF16)
        for r in range(sites):
            xs[r, span * b : span * (b + 1), :] = rows[span * r : span * (r + 1)]

    half = seqs // 2
    order = one_hot(
        seqs, seqs,
        lambda o, k: k == ((o % half) // 2) * 4 + (o // half) * 2 + o % 2,
    )
    order = (order * chain_ref[...].astype(F32)).astype(BF16)
    present = present_ref[...].astype(F32)
    live = jnp.dot(order, present.astype(BF16), preferred_element_type=F32).astype(BF16)
    select = one_hot(
        residues, pack, lambda j, c: j == place * sites + c // OUTER_CHANNELS
    ).astype(BF16)
    select_t = one_hot(
        pack, residues, lambda c, j: j == place * sites + c % sites
    ).astype(BF16)
    live_l = jnp.dot(live, select, preferred_element_type=F32)
    live_r = contract_lanes(select_t, live)
    keep[...] = live_r[:8]
    live_t = contract_lanes(present.T.astype(BF16), order).astype(BF16)
    counts = jnp.dot(live_t, live_l.astype(BF16), preferred_element_type=F32)
    inverse_ref[...] = 1.0 / jnp.maximum(counts, 1.0)

    head_of_lane = lax.broadcasted_iota(jnp.int32, (1, inner), 1) // HEAD_CHANNELS
    left_sum[...] = jnp.zeros_like(left_sum)
    right_sum[...] = jnp.zeros_like(right_sum)

    def one_site(r, carry):
        x = xs[r].astype(F32)
        normed = normalize(x, gain_ref[...], offset_ref[...])
        query_key = jnp.dot(normed, qk_ref[...], preferred_element_type=F32)
        value_gate = jnp.dot(normed, vg_ref[...], preferred_element_type=F32)
        query = (query_key[:, :inner] * HEAD_CHANNELS ** (-0.5)).astype(BF16)
        key = query_key[:, inner:].astype(BF16)
        value = value_gate[:, :inner].astype(BF16)
        gate = jax.nn.sigmoid(value_gate[:, inner:] + gate_ref[...])
        alive = keep[pl.ds(r, 1), :] > 0
        mixed = jnp.zeros((seqs, inner), F32)
        for h in range(HEAD_COUNT):
            own = head_of_lane == h
            query_h = query * own.astype(F32).astype(BF16)
            scores = jnp.where(alive, contract_lanes(query_h, key), MASKED)
            exponent = jnp.exp(scores - jnp.max(scores, axis=-1, keepdims=True))
            total = jnp.sum(exponent, axis=-1, keepdims=True)
            part = jnp.dot(exponent.astype(BF16), value, preferred_element_type=F32)
            mixed = jnp.where(own, part * (1.0 / total), mixed)
        gated = (mixed * gate).astype(BF16)
        update = jnp.dot(gated, exit_ref[...], preferred_element_type=F32) + exit_add_ref[...]
        after = (x + update).astype(BF16)
        ys[r] = after
        again = normalize(after.astype(F32), gain2_ref[...], offset2_ref[...])
        channels = 2 * OUTER_CHANNELS
        spread_l = one_hot(
            pack, channels,
            lambda o, c: (c == o % OUTER_CHANNELS) & (o // OUTER_CHANNELS == r),
        ).astype(BF16)
        spread_r = one_hot(
            pack, channels,
            lambda o, c: (c == OUTER_CHANNELS + o // sites) & (o % sites == r),
        ).astype(BF16)
        twin_l = jnp.dot(spread_l, twin_ref[...], preferred_element_type=F32).astype(BF16)
        twin_r = jnp.dot(spread_r, twin_ref[...], preferred_element_type=F32).astype(BF16)
        left_sum[...] += contract_lanes(again, twin_l)
        right_sum[...] += contract_lanes(twin_r, again)
        return carry

    lax.fori_loop(0, sites, one_site, 0)
    channels = 2 * OUTER_CHANNELS
    shift = shift_ref[...]
    across = one_hot(pack, channels, lambda o, c: c == OUTER_CHANNELS + o // sites)
    shift_r = jnp.sum(across * shift, axis=1, keepdims=True)
    column = jnp.sum(
        one_hot(channels, channels, lambda a, c: a == c) * shift, axis=1, keepdims=True
    )
    down = one_hot(channels, pack, lambda c, o: c == o % OUTER_CHANNELS)
    shift_l = jnp.sum(down * column, axis=0, keepdims=True)
    left_ref[...] = ((left_sum[...] + shift_l) * live_l).astype(BF16)
    right_ref[...] = ((right_sum[...] + shift_r) * live_r).astype(BF16)

    group = 2 * span
    place_back = one_hot(
        group * sites, group * sites,
        lambda o, k: k
        == (
            ((o % sites) * 2 + (o // (2 * sites)) % 2) * span
            + (o // (4 * sites)) * 2
            + (o // sites) % 2
        ),
    ).astype(BF16)
    for g in range(seqs // group):
        stack = jnp.concatenate(
            [
                ys[r, half * c + span * g : half * c + span * (g + 1), :]
                for r in range(sites)
                for c in range(2)
            ],
            axis=0,
        )
        rows = jnp.dot(place_back, stack, preferred_element_type=F32).astype(BF16)
        after_ref[group * g : group * (g + 1)] = rows.reshape(group, sites, width)


def attend(place, x, present, *rest):
    seqs, residues = present.shape
    width = x.shape[1]
    sites = x.shape[0] // (2 * seqs)
    pack = sites * OUTER_CHANNELS
    vmem = pl.BlockSpec(memory_space=pltpu.VMEM)
    return pl.pallas_call(
        attend_kernel,
        out_shape=(
            jax.ShapeDtypeStruct((seqs, sites, width), BF16),
            jax.ShapeDtypeStruct((seqs, pack), BF16),
            jax.ShapeDtypeStruct((pack, seqs), BF16),
            jax.ShapeDtypeStruct((residues, pack), F32),
        ),
        in_specs=[pl.BlockSpec(memory_space=pltpu.SMEM)] + [vmem] * (2 + len(rest)),
        out_specs=(vmem,) * 4,
        scratch_shapes=[
            pltpu.VMEM((sites, seqs, width), BF16),
            pltpu.VMEM((sites, seqs, width), BF16),
            pltpu.VMEM((8, seqs), F32),
            pltpu.VMEM((seqs, pack), F32),
            pltpu.VMEM((pack, seqs), F32),
        ],
        compiler_params=pltpu.CompilerParams(vmem_limit_bytes=VMEM_LIMIT),
        name="attend",
    )(place, x, present, *rest)


def pair_kernel(right_ref, left_ref, inverse_ref, couple_ref, shift_ref, out_ref, terms, blocks, wide):
    step = pl.program_id(0)
    owners, pack, seqs = right_ref.shape
    sites = out_ref.shape[0]
    chip_rows = 2 * sites
    halves = OUTER_CHANNELS // 2

    @pl.when(step == 0)
    def _():
        wide[...] = couple_ref[...].astype(F32)
        blocks[...] = jnp.zeros_like(blocks)
        for e in range(OUTER_CHANNELS):
            part = wide[pl.ds(e, OUTER_CHANNELS, stride=OUTER_CHANNELS), :].astype(BF16)
            for i in range(sites):
                row = e * pack + i * OUTER_CHANNELS
                blocks[row : row + OUTER_CHANNELS, i * PAIR_DIM : (i + 1) * PAIR_DIM] = part

    lower = lax.broadcasted_iota(jnp.int32, (1, chip_rows, 1), 1) < sites
    left = left_ref[...]

    def four(u, carry):
        quad = right_ref[pl.ds(4 * u, 4)].reshape(4 * pack, seqs)
        sums = jnp.dot(quad, left, preferred_element_type=F32)
        sums = sums.reshape(4, halves, chip_rows, pack)
        even, odd = [], []
        for t in range(2):
            a, b = sums[2 * t], sums[2 * t + 1]
            first = pl.multiple_of((step * owners + 4 * u + 2 * t) * sites, chip_rows)
            scale = inverse_ref[pl.ds(first, chip_rows), :][None]
            even.append(jnp.where(lower, a, pltpu.roll(b, sites, 1)) * scale)
            odd.append(jnp.where(lower, pltpu.roll(a, sites, 1), b) * scale)
        rows = pl.ds(pl.multiple_of((step * owners + 4 * u) * sites, 2 * chip_rows), 2 * chip_rows)
        even = jnp.concatenate(even, axis=1).astype(BF16)
        odd = jnp.concatenate(odd, axis=1).astype(BF16)
        for e in range(halves):
            terms[rows, 2 * e * pack : (2 * e + 1) * pack] = even[e]
            terms[rows, (2 * e + 1) * pack : (2 * e + 2) * pack] = odd[e]
        return carry

    lax.fori_loop(0, owners // 4, four, 0)

    @pl.when(step == pl.num_programs(0) - 1)
    def _():
        total = jnp.dot(terms[...], blocks[...], preferred_element_type=F32)
        for i in range(sites):
            part = total[:, i * PAIR_DIM : (i + 1) * PAIR_DIM] + shift_ref[...]
            out_ref[i] = part.astype(BF16)


def pairs(right_all, left, inverse, couple, shift):
    owners, pack, seqs = right_all.shape
    residues = inverse.shape[0]
    sites = pack // OUTER_CHANNELS
    steps = 4
    whole = lambda *shape: pl.BlockSpec(shape, lambda g: (0,) * len(shape))
    return pl.pallas_call(
        pair_kernel,
        grid=(steps,),
        in_specs=[
            pl.BlockSpec((owners // steps, pack, seqs), lambda g: (g, 0, 0)),
            whole(*left.shape),
            whole(*inverse.shape),
            whole(*couple.shape),
            whole(*shift.shape),
        ],
        out_specs=whole(sites, residues, PAIR_DIM),
        out_shape=jax.ShapeDtypeStruct((sites, residues, PAIR_DIM), BF16),
        scratch_shapes=[
            pltpu.VMEM((residues, OUTER_CHANNELS * pack), BF16),
            pltpu.VMEM((OUTER_CHANNELS * pack, sites * PAIR_DIM), BF16),
            pltpu.VMEM(couple.shape, F32),
        ],
        compiler_params=pltpu.CompilerParams(
            vmem_limit_bytes=VMEM_LIMIT, dimension_semantics=("arbitrary",)
        ),
        name="pairs",
    )(right_all, left, inverse, couple, shift)


def exchange_kernel(size, x_ref, out_ref, sent, got, swap_send, swap_got, own_sem):
    y, x, core = (lax.axis_index(a) for a in DAP)
    chips = size * size
    partner = {"dap_2": 1 - core}
    here = y * size + x
    far = size // 2
    steps = [(dy, dx) for dy in range(size) for dx in range(size) if dy or dx]
    away = lambda d: min(d, size - d)
    steps.sort(key=lambda d: -(away(d[0]) + away(d[1])))
    mesh = pl.DeviceIdType.MESH

    def chip(step):
        return lax.rem(y + step[0], size), lax.rem(x + step[1], size)

    own = pltpu.make_async_copy(x_ref.at[:, here], out_ref.at[core, here], own_sem)
    own.start()
    barrier = pltpu.get_barrier_semaphore()
    for step in steps:
        row, column = chip(step)
        pl.semaphore_signal(
            barrier, inc=1, device_id={"dap_0": row, "dap_1": column}, device_id_type=mesh
        )
    pl.semaphore_signal(barrier, inc=1, device_id=partner, device_id_type=mesh)
    pl.semaphore_wait(barrier, chips)
    for step in steps:
        row, column = chip(step)
        pltpu.make_async_remote_copy(
            src_ref=x_ref.at[:, row * size + column], dst_ref=out_ref.at[core, here],
            send_sem=sent, recv_sem=got, device_id={"dap_0": row, "dap_1": column},
            device_id_type=mesh,
        ).start()
    own.wait()
    others = out_ref.at[core, pl.ds(0, chips - 1)]
    pltpu.make_async_copy(others, others, got).wait()
    swap = pltpu.make_async_remote_copy(
        src_ref=out_ref.at[core], dst_ref=out_ref.at[core], send_sem=swap_send,
        recv_sem=swap_got, device_id=partner, device_id_type=mesh,
    )
    swap.start()
    pltpu.make_async_copy(others, others, sent).wait()
    swap.wait()


def exchange(x, size):
    seqs, residues, width = x.shape
    chips = size * size
    x = x.reshape(seqs, chips, residues // chips, width)
    out = pl.pallas_call(
        functools.partial(exchange_kernel, size),
        out_shape=jax.ShapeDtypeStruct((2, chips, seqs, residues // chips, width), x.dtype),
        in_specs=[pl.BlockSpec(memory_space=pl.ANY)],
        out_specs=pl.BlockSpec(memory_space=pl.ANY),
        scratch_shapes=[pltpu.SemaphoreType.DMA] * 5,
        compiler_params=pltpu.CompilerParams(
            vmem_limit_bytes=VMEM_LIMIT, collective_id=2, has_side_effects=True
        ),
        name="exchange",
    )(x)
    return out.reshape(2 * seqs * residues, width)


GATHER_RING = pltpu.CompilerParams(
    vmem_limit_bytes=VMEM_LIMIT, collective_id=1, has_side_effects=True
)


def ring_order(size):
    far = size // 2
    offsets = [0]
    for hop in range(1, far):
        offsets += [-hop, hop]
    offsets.append(far)
    events = []
    for offset in offsets:
        ready = 2.6 + 1.4 * abs(offset) if offset else 0.0
        if offset:
            events.append((ready, 0, 0, offset))
        for hop in range(1, far + 1):
            events.append((ready + 3.3 * hop + 0.01, 1, hop, offset))
    return sorted(events, key=lambda event: event[:2]), offsets


def gather_kernel(size, own_ref, all_ref, held, p_recv, s_recv, x_recv, send_sem, out_sem, in_sem):
    far = size // 2
    y, x, core = (lax.axis_index(a) for a in DAP)
    half = own_ref.shape[0] // 2

    def at(first, second):
        row = jnp.where(core == 0, second, first)
        column = jnp.where(core == 0, first, second)
        return lax.rem(row + size, size), lax.rem(column + size, size)

    main = jnp.where(core == 0, x, y)
    side = jnp.where(core == 0, y, x)

    def device(first, second):
        row, column = at(first, second)
        return {"dap_0": row, "dap_1": column}

    def slot(first, second, which):
        row, column = at(first, second)
        return (row * size + column) * 2 + which

    partner = {"dap_2": 1 - core}
    events, offsets = ring_order(size)
    neighbours = [device(main + offset, side) for offset in offsets if offset]
    neighbours += [device(main, side + 1), device(main, side - 1), partner]
    barrier = pltpu.get_barrier_semaphore()
    own_copy = pltpu.make_async_copy(own_ref, held.at[slot(main, side, core)], in_sem)
    own_copy.start()
    for neighbour in neighbours:
        pl.semaphore_signal(
            barrier, inc=1, device_id=neighbour, device_id_type=pl.DeviceIdType.MESH
        )
    pl.semaphore_wait(barrier, len(neighbours))
    own_copy.wait()

    def piece(first, second, which, hop, sign):
        ref = held.at[slot(first, second, which)]
        if hop < far:
            return ref
        return ref.at[pl.ds(0 if sign > 0 else half, half)]

    def remote(ref, recv, target):
        return pltpu.make_async_remote_copy(
            src_ref=ref, dst_ref=ref, send_sem=send_sem, recv_sem=recv,
            device_id=target, device_id_type=pl.DeviceIdType.MESH,
        )

    def along_main(offset):
        ref = held.at[slot(main, side, core)]
        remote(ref, p_recv.at[offsets.index(offset)], device(main - offset, side)).start()

    def along_side(offset, index, hop, sign):
        ref = piece(main + offset, side - sign * (hop - 1), core, hop, sign)
        remote(ref, s_recv.at[index, (sign + 1) // 2, hop - 1], device(main, side + sign)).start()

    def finished(first, second, order):
        ref = held.at[slot(first, second, core)]
        remote(ref, x_recv.at[order], partner).start()
        pltpu.make_async_copy(ref, all_ref.at[slot(first, second, core)], out_sem).start()
        done.append((first, second))

    def from_partner(order):
        first, second = done[order]
        ref = held.at[swapped_slot(first, second)]
        remote(ref, x_recv.at[order], partner).wait_recv()
        pltpu.make_async_copy(ref, all_ref.at[swapped_slot(first, second)], out_sem).start()

    def swapped_slot(first, second):
        d_first, d_second = first - main, second - side
        row = jnp.where(core == 0, main_row + d_first, main_row + d_second)
        column = jnp.where(core == 0, main_column + d_second, main_column + d_first)
        row, column = lax.rem(row + size, size), lax.rem(column + size, size)
        return (row * size + column) * 2 + (1 - core)

    main_row, main_column = y, x
    done = []
    for sign in (1, -1):
        along_side(0, 0, 1, sign)
    for offset in offsets:
        if offset:
            along_main(offset)
    finished(main, side, 0)
    lag, taken = 6, 0
    for _, kind, hop, offset in events:
        index = offsets.index(offset)
        if kind == 0:
            ref = held.at[slot(main + offset, side, core)]
            remote(ref, p_recv.at[index], partner).wait_recv()
            for way in (1, -1):
                along_side(offset, index, 1, way)
            finished(main + offset, side, len(done))
        else:
            for sign in (1, -1):
                ref = piece(main + offset, side - sign * hop, core, hop, sign)
                remote(ref, s_recv.at[index, (sign + 1) // 2, hop - 1], partner).wait_recv()
                if hop < far:
                    along_side(offset, index, hop + 1, sign)
                    finished(main + offset, side - sign * hop, len(done))
            if hop == far:
                finished(main + offset, side + far, len(done))
        while taken < len(done) - lag:
            from_partner(taken)
            taken += 1
    while taken < len(done):
        from_partner(taken)
        taken += 1
    sent = (size - 1) * (size + 1) + size * size
    drained = held.at[pl.ds(0, sent)]
    pltpu.make_async_copy(drained, drained, send_sem).wait()
    pltpu.make_async_copy(held, all_ref, out_sem).wait()


def gather_right(own, size):
    owners = 2 * size * size
    return pl.pallas_call(
        functools.partial(gather_kernel, size),
        out_shape=jax.ShapeDtypeStruct((owners, *own.shape), own.dtype),
        in_specs=[pl.BlockSpec(memory_space=pl.ANY)],
        out_specs=pl.BlockSpec(memory_space=pl.ANY),
        scratch_shapes=[
            pltpu.VMEM((owners, *own.shape), own.dtype),
            pltpu.SemaphoreType.DMA((size,)),
            pltpu.SemaphoreType.DMA((size, 2, size // 2)),
            pltpu.SemaphoreType.DMA((size * size,)),
            pltpu.SemaphoreType.DMA,
            pltpu.SemaphoreType.DMA,
            pltpu.SemaphoreType.DMA,
        ],
        compiler_params=GATHER_RING,
        name="gather_right",
    )(own)


def shards(
    homolog_stack_tensor,
    occupancy_indicator,
    chain_existence_flags,
    focus_normal_factor,
    focus_normal_addend,
    probe_index_weights,
    payload_valve_weights,
    logistic_valve_addend,
    focus_exit_weights,
    focus_exit_addend,
    product_mean_layer_stretch,
    product_mean_layer_shift,
    twin_map_matrix,
    twin_map_shift,
    couple_map_matrix,
    couple_map_shift,
):
    seqs, residues = occupancy_indicator.shape
    width = homolog_stack_tensor.shape[-1]
    size = lax.axis_size("dap_0")
    row = lambda v: v[None, :]
    after, left, right, inverse = attend(
        lax.axis_index(DAP)[None],
        exchange(homolog_stack_tensor, size),
        occupancy_indicator,
        row(chain_existence_flags),
        row(focus_normal_factor),
        row(focus_normal_addend),
        probe_index_weights,
        payload_valve_weights,
        row(logistic_valve_addend),
        focus_exit_weights,
        row(focus_exit_addend),
        row(product_mean_layer_stretch),
        row(product_mean_layer_shift),
        twin_map_matrix.T,
        row(twin_map_shift),
    )
    right_all = gather_right(right, size)
    pair_rows = pairs(right_all, left, inverse, couple_map_matrix, row(couple_map_shift))
    return (after, pair_rows)


def solution(mesh):
    split = Mesh(
        mesh.devices.reshape(mesh.shape["grp"], 8, 8, 2), ("grp", "dap_0", "dap_1", "dap_2")
    )
    return jax.shard_map(
        shards,
        mesh=split,
        in_specs=(
            P(GRP_DAP, None, None),
            P("grp", None),
            P("grp"),
            P(),
            P(),
            P(),
            P(),
            P(),
            P(),
            P(),
            P(),
            P(),
            P(),
            P(),
            P(),
            P(),
        ),
        out_specs=(P("grp", DAP, None), P(GRP_DAP, None, None)),
        check_vma=False,
    )
```

time: 117 us -> 97.3 us (0.83)
  Pallas kernels: 62.2 us -> 96.5 us
  blocking collectives: 24.2 us -> 0 us
  local copies, waits for them, and re-layouts: 16.6 us -> 0 us
  starting transfers between devices: 6.49 us -> 0 us
  waiting for transfers between devices: 5.04 us -> 0 us
  other arithmetic: 1.47 us -> 0 us
    pallas_call x1 -> x2, Pallas kernels: 9.32 us -> 47.2 us  [the longest x1 36.4 us: exchange(): pl.pallas_call(functools.partial(exchange_kernel, size), out_shape=jax.Sh...]
    all_to_all x1 -> x0, blocking collectives: 24.2 us -> none  [exchange_in_order(): lax.all_to_all(parts, axes[k], split_axis=k, concat_axis=k, tiled=True)]
    all_to_all x1 -> x0, starting transfers between devices: 6.49 us -> none  [exchange_in_order(): lax.all_to_all(parts, axes[k], split_axis=k, concat_axis=k, tiled=True)]
    all_to_all x1 -> x0, waiting for transfers between devices: 5.04 us -> none  [exchange_in_order(): lax.all_to_all(parts, axes[k], split_axis=k, concat_axis=k, tiled=True)]
    reshape x4 -> x0, local copies, waits for them, and re-layouts: 4.13 us -> none  [the longest x1 1.77 us: shards(): couple_map_matrix.reshape(OUTER_CHANNELS, OUTER_CHANNELS, PAIR_DIM)]
    pallas_call x1, Pallas kernels: 40.1 us -> 36.1 us  [gather_right(): pl.pallas_call(functools.partial(gather_kernel, size), out_shape=jax.Shap...]
    another operation x8 -> x0, local copies, waits for them, and re-layouts: 3.79 us -> none  [the longest x1 0.99 us: joined_along(): parts.reshape(*shape[:dim], shape[dim] * shape[dim + 1], *shape[dim + 2:])]
    unnamed x2 -> x0, local copies, waits for them, and re-layouts: 3.48 us -> none
  transfers between devices with their start and end apart: 1 -> 0, of which waited for: 1 -> 0; matrix products, arithmetic and copies ran while one was open for 10% -> 0% of each run, Pallas kernels for 0% -> 0%
where the time goes in v2:
time: 97.3 us; the launch traced here: 97.2 us
  Pallas kernels  96.5 us (99%)
    pallas_call x1, Pallas kernels, exchange(): pl.pallas_call(functools.partial(exchange_kernel, size), out_shape=jax.Sh...  36.4 us
    pallas_call x1, Pallas kernels, gather_right(): pl.pallas_call(functools.partial(gather_kernel, size), out_shape=jax.Shap...  36.1 us
    pallas_call x1, Pallas kernels, pairs(): pl.pallas_call(pair_kernel, grid=(steps,), in_specs=[pl.BlockSpec((owners...  13.2 us
    pallas_call x1, Pallas kernels, attend(): pl.pallas_call(attend_kernel, out_shape=(jax.ShapeDtypeStruct((seqs, site...  10.8 us

profile of v2, /device:TPU:513, one launch (start us, length us, event | category | flops | bytes accessed | tf_op | source)
XLA Modules:
  0.0 97.2 jit_solution(409413926784066762)
XLA Ops:
  0.6 36.4 %exchange.1 = bf16[2,64,2,8,256]{4,3,2,1,0:T(8,128)(2,1)} custom-call(bf16[2,64,8,256]{3,2,1,0:T(8,128)(2,1)} %bitcast.14), custom_call_target="tpu_custom_call" | custom-call | tf_op jit(solution)/shard_map/exchange/pallas_call | solution.py:323
  37.1 10.8 %attend.1 = (bf16[256,4,256]{2,1,0:T(4,128)(2,1)}, bf16[256,128]{1,0:T(8,128)(2,1)}, bf16[128,256]{1,0:T(8,128)(2,1)}, f32[512,128]{1,0:T(8,128)}) custom-call(s32[1]{0:T(128)} %bitcast.place_ref, bf16[2048,256]{1,0:T(8,128)(2,1)} %bitcast.13, s32[256,512]{1,0:T(8,128)} %present_ref.1, s32[1,256]{1,0:T(1,128)} %bitcast.16, f32[1,256]{1,0:T(1,128)} %bitcast.17, ...), custom_call_target="tpu_custom_call" | custom-call | tf_op jit(solution)/shard_map/attend/pallas_call | solution.py:175
  47.9 36.1 %gather_right.1.right_ref = bf16[128,128,256]{2,1,0:T(8,128)(2,1)} custom-call(bf16[128,256]{1,0:T(8,128)(2,1)} %get-tuple-element.7.own_ref), custom_call_target="tpu_custom_call" | custom-call | tf_op jit(solution)/shard_map/gather_right/pallas_call | solution.py:472
  84.0 13.2 %pairs.1 = bf16[4,512,128]{2,1,0:T(8,128)(2,1)} custom-call(bf16[128,128,256]{2,1,0:T(8,128)(2,1)} %gather_right.1.right_ref, bf16[256,128]{1,0:T(8,128)(2,1)} %get-tuple-element.8.left_ref, f32[512,128]{1,0:T(8,128)} %get-tuple-element.9.inverse_ref, bf16[1024,128]{1,0:T(8,128)(2,1)} %couple_ref.1, f32[1,128]{1,0:T(1,128)} %bitcast.24), custom_call_target="tpu_custom_call" | custom-call | tf_op jit(solution)/shard_map/pairs/pallas_call | solution.py:252

commit v3 on v2

--- a/solution.py
+++ b/solution.py
@@ -194,83 +194,252 @@
     )(place, x, present, *rest)
 
 
-def pair_kernel(right_ref, left_ref, inverse_ref, couple_ref, shift_ref, out_ref, terms, blocks, wide):
-    step = pl.program_id(0)
-    owners, pack, seqs = right_ref.shape
+def ring_order(size):
+    far = size // 2
+    offsets = [0]
+    for hop in range(1, far):
+        offsets += [-hop, hop]
+    offsets.append(far)
+    first = {0: 0.0, 1: 4.0, 2: 5.4}
+    events = []
+    for offset in offsets:
+        hop = abs(offset)
+        ready = first.get(hop, 5.4 + 3.3 * (hop - 2) - 2.6 * (hop - 3))
+        if offset:
+            events.append((ready, 0, 0, offset))
+        for hop in range(1, far + 1):
+            events.append((ready + 3.3 * hop + 0.01, 1, hop, offset))
+    return sorted(events, key=lambda event: event[:2]), offsets
+
+
+def pair_kernel(
+    size, own_ref, left_ref, inverse_ref, couple_ref, shift_ref, out_ref,
+    held, terms, blocks, wide, total, couple, left, inverse,
+    p_recv, s_recv, x_recv, send_sem, in_sem,
+):
+    far = size // 2
+    chips = size * size
+    y, x, core = (lax.axis_index(a) for a in DAP)
+    pack = own_ref.shape[0]
+    half = pack // 2
     sites = out_ref.shape[0]
     chip_rows = 2 * sites
     halves = OUTER_CHANNELS // 2
-
-    @pl.when(step == 0)
-    def _():
-        wide[...] = couple_ref[...].astype(F32)
-        blocks[...] = jnp.zeros_like(blocks)
-        for e in range(OUTER_CHANNELS):
-            part = wide[pl.ds(e, OUTER_CHANNELS, stride=OUTER_CHANNELS), :].astype(BF16)
-            for i in range(sites):
-                row = e * pack + i * OUTER_CHANNELS
-                blocks[row : row + OUTER_CHANNELS, i * PAIR_DIM : (i + 1) * PAIR_DIM] = part
+    mesh = pl.DeviceIdType.MESH
+
+    def at(first, second):
+        row = jnp.where(core == 0, second, first)
+        column = jnp.where(core == 0, first, second)
+        return lax.rem(row + size, size), lax.rem(column + size, size)
+
+    main = jnp.where(core == 0, x, y)
+    side = jnp.where(core == 0, y, x)
+
+    def device(first, second):
+        row, column = at(first, second)
+        return {"dap_0": row, "dap_1": column}
+
+    def chip(first, second):
+        row, column = at(main + first, side + second)
+        return row * size + column
+
+    def slot(first, second):
+        return chip(first, second) * 2 + core
+
+    events, offsets = ring_order(size)
+    partner = {"dap_2": 1 - core}
+    neighbours = [device(main + step, side) for step in (1, -1, 2, -2)]
+    neighbours += [device(main, side + 1), device(main, side - 1), partner]
+    own_copy = pltpu.make_async_copy(own_ref, held.at[slot(0, 0)], in_sem.at[0])
+    own_copy.start()
+    loads = [
+        pltpu.make_async_copy(a, b, in_sem.at[1 + i])
+        for i, (a, b) in enumerate(
+            ((couple_ref, couple), (left_ref, left), (inverse_ref, inverse))
+        )
+    ]
+    for load in loads:
+        load.start()
+    barrier = pltpu.get_barrier_semaphore()
+    for neighbour in neighbours:
+        pl.semaphore_signal(barrier, inc=1, device_id=neighbour, device_id_type=mesh)
+    pl.semaphore_wait(barrier, len(neighbours))
+    own_copy.wait()
+
+    def part(ref, sign):
+        return ref.at[pl.ds(0 if sign > 0 else half, half)]
+
+    def remote(ref, recv, target):
+        return pltpu.make_async_remote_copy(
+            src_ref=ref, dst_ref=ref, send_sem=send_sem, recv_sem=recv,
+            device_id=target, device_id_type=mesh,
+        )
+
+    def main_sem(offset, sign):
+        return p_recv.at[offsets.index(offset) + (1 if offset == far and sign < 0 else 0)]
+
+    def along_main(origin, sign, step):
+        reach = origin - sign * step
+        ref = held.at[slot(origin, 0)]
+        if abs(reach) == far:
+            reach, ref = far, part(ref, sign)
+        remote(ref, main_sem(reach, sign), device(main + sign * step, side)).start()
+
+    def along_side(offset, hop, sign):
+        ref = held.at[slot(offset, -sign * (hop - 1))]
+        if hop == far:
+            ref = part(ref, sign)
+        recv = s_recv.at[offsets.index(offset), (sign + 1) // 2, hop - 1]
+        remote(ref, recv, device(main, side + sign)).start()
+
+    def reduced(second):
+        return second if second > -far else far
+
+    done = []
+
+    def finished(first, second):
+        remote(held.at[slot(first, second)], x_recv.at[len(done)], partner).start()
+        done.append((first, reduced(second)))
+
+    for sign in (1, -1):
+        along_side(0, 1, sign)
+    for step in (2, 1):
+        for sign in (1, -1):
+            along_main(0, sign, step)
+    finished(0, 0)
+
+    for load in loads:
+        load.wait()
+    wide[...] = couple[...].astype(F32)
+    blocks[...] = jnp.zeros_like(blocks)
+    for e in range(OUTER_CHANNELS):
+        rows = wide[pl.ds(e, OUTER_CHANNELS, stride=OUTER_CHANNELS), :].astype(BF16)
+        for i in range(sites):
+            row = e * pack + i * OUTER_CHANNELS
+            blocks[row : row + OUTER_CHANNELS, i * PAIR_DIM : (i + 1) * PAIR_DIM] = rows
 
     lower = lax.broadcasted_iota(jnp.int32, (1, chip_rows, 1), 1) < sites
-    left = left_ref[...]
-
-    def four(u, carry):
-        quad = right_ref[pl.ds(4 * u, 4)].reshape(4 * pack, seqs)
-        sums = jnp.dot(quad, left, preferred_element_type=F32)
+
+    def from_partner(first, second):
+        ref = held.at[chip(first, second) * 2 + (1 - core)]
+        remote(ref, x_recv.at[done.index((second, first))], partner).wait_recv()
+
+    def multiply(unit, members):
+        quad = []
+        for member in members:
+            from_partner(*member)
+            first = chip(*member) * 2
+            quad += [held[first], held[first + 1]]
+        sums = jnp.dot(jnp.concatenate(quad, axis=0), left[...], preferred_element_type=F32)
         sums = sums.reshape(4, halves, chip_rows, pack)
         even, odd = [], []
-        for t in range(2):
+        for t, member in enumerate(members):
             a, b = sums[2 * t], sums[2 * t + 1]
-            first = pl.multiple_of((step * owners + 4 * u + 2 * t) * sites, chip_rows)
-            scale = inverse_ref[pl.ds(first, chip_rows), :][None]
+            first = pl.multiple_of(chip(*member) * chip_rows, chip_rows)
+            scale = inverse[pl.ds(first, chip_rows), :][None]
             even.append(jnp.where(lower, a, pltpu.roll(b, sites, 1)) * scale)
             odd.append(jnp.where(lower, pltpu.roll(a, sites, 1), b) * scale)
-        rows = pl.ds(pl.multiple_of((step * owners + 4 * u) * sites, 2 * chip_rows), 2 * chip_rows)
+        rows = slice(2 * chip_rows * unit, 2 * chip_rows * (unit + 1))
         even = jnp.concatenate(even, axis=1).astype(BF16)
         odd = jnp.concatenate(odd, axis=1).astype(BF16)
         for e in range(halves):
             terms[rows, 2 * e * pack : (2 * e + 1) * pack] = even[e]
             terms[rows, (2 * e + 1) * pack : (2 * e + 2) * pack] = odd[e]
-        return carry
-
-    lax.fori_loop(0, owners // 4, four, 0)
-
-    @pl.when(step == pl.num_programs(0) - 1)
-    def _():
-        total = jnp.dot(terms[...], blocks[...], preferred_element_type=F32)
-        for i in range(sites):
-            part = total[:, i * PAIR_DIM : (i + 1) * PAIR_DIM] + shift_ref[...]
-            out_ref[i] = part.astype(BF16)
-
-
-def pairs(right_all, left, inverse, couple, shift):
-    owners, pack, seqs = right_all.shape
+
+    placed = []
+
+    def project(first, count):
+        rows = slice(chip_rows * first, chip_rows * (first + count))
+        result = jnp.dot(terms[rows, :], blocks[...], preferred_element_type=F32)
+        for k in range(count):
+            row = pl.multiple_of(chip(*placed[first + k]) * chip_rows, chip_rows)
+            total[pl.ds(row, chip_rows), :] = result[chip_rows * k : chip_rows * (k + 1)]
+
+    def advance(lag):
+        while True:
+            ready = [
+                (max(done.index(m), done.index(m[::-1])), m)
+                for m in done
+                if m not in placed and m[::-1] in done
+            ]
+            ready = [m for at, m in sorted(ready) if at < len(done) - lag]
+            if len(ready) < 2:
+                return
+            multiply(len(placed) // 2, ready[:2])
+            placed.extend(ready[:2])
+            if len(placed) == chips // 2:
+                project(0, chips // 2)
+
+    for _, kind, hop, offset in events:
+        if kind == 0:
+            ref = held.at[slot(offset, 0)]
+            if offset == far:
+                for sign in (1, -1):
+                    remote(part(ref, sign), main_sem(far, sign), partner).wait_recv()
+            else:
+                remote(ref, main_sem(offset, 1), partner).wait_recv()
+            if abs(offset) == 2:
+                sign = -offset // 2
+                along_main(offset, sign, 2)
+                along_main(offset, sign, 1)
+            for way in (1, -1):
+                along_side(offset, 1, way)
+            finished(offset, 0)
+        else:
+            for sign in (1, -1):
+                ref = held.at[slot(offset, -sign * hop)]
+                if hop == far:
+                    ref = part(ref, sign)
+                recv = s_recv.at[offsets.index(offset), (sign + 1) // 2, hop - 1]
+                remote(ref, recv, partner).wait_recv()
+                if hop < far:
+                    along_side(offset, hop + 1, sign)
+                    finished(offset, -sign * hop)
+            if hop == far:
+                finished(offset, far)
+        advance(5)
+    advance(0)
+    project(chips // 2, chips // 2)
+    for i in range(sites):
+        rows = total[:, i * PAIR_DIM : (i + 1) * PAIR_DIM] + shift_ref[...]
+        out_ref[i] = rows.astype(BF16)
+    sent = (size - 1) * (size + 1) + size * size
+    drained = held.at[pl.ds(0, sent)]
+    pltpu.make_async_copy(drained, drained, send_sem).wait()
+
+
+def pairs(right, left, inverse, couple, shift, size):
+    pack, seqs = right.shape
     residues = inverse.shape[0]
+    owners = 2 * size * size
     sites = pack // OUTER_CHANNELS
-    steps = 4
-    whole = lambda *shape: pl.BlockSpec(shape, lambda g: (0,) * len(shape))
+    hbm = pl.BlockSpec(memory_space=pl.ANY)
+    vmem = pl.BlockSpec(memory_space=pltpu.VMEM)
     return pl.pallas_call(
-        pair_kernel,
-        grid=(steps,),
-        in_specs=[
-            pl.BlockSpec((owners // steps, pack, seqs), lambda g: (g, 0, 0)),
-            whole(*left.shape),
-            whole(*inverse.shape),
-            whole(*couple.shape),
-            whole(*shift.shape),
-        ],
-        out_specs=whole(sites, residues, PAIR_DIM),
+        functools.partial(pair_kernel, size),
+        in_specs=[hbm, hbm, hbm, hbm, vmem],
+        out_specs=vmem,
         out_shape=jax.ShapeDtypeStruct((sites, residues, PAIR_DIM), BF16),
         scratch_shapes=[
+            pltpu.VMEM((owners, pack, seqs), BF16),
             pltpu.VMEM((residues, OUTER_CHANNELS * pack), BF16),
             pltpu.VMEM((OUTER_CHANNELS * pack, sites * PAIR_DIM), BF16),
             pltpu.VMEM(couple.shape, F32),
+            pltpu.VMEM((residues, sites * PAIR_DIM), F32),
+            pltpu.VMEM(couple.shape, BF16),
+            pltpu.VMEM(left.shape, BF16),
+            pltpu.VMEM(inverse.shape, F32),
+            pltpu.SemaphoreType.DMA((size + 1,)),
+            pltpu.SemaphoreType.DMA((size, 2, size // 2)),
+            pltpu.SemaphoreType.DMA((size * size,)),
+            pltpu.SemaphoreType.DMA,
+            pltpu.SemaphoreType.DMA((4,)),
         ],
         compiler_params=pltpu.CompilerParams(
-            vmem_limit_bytes=VMEM_LIMIT, dimension_semantics=("arbitrary",)
+            vmem_limit_bytes=VMEM_LIMIT, collective_id=1, has_side_effects=True
         ),
         name="pairs",
-    )(right_all, left, inverse, couple, shift)
+    )(right, left, inverse, couple, shift)
 
 
 def exchange_kernel(size, x_ref, out_ref, sent, got, swap_send, swap_got, own_sem):
@@ -527,8 +696,7 @@
         twin_map_matrix.T,
         row(twin_map_shift),
     )
-    right_all = gather_right(right, size)
-    pair_rows = pairs(right_all, left, inverse, couple_map_matrix, row(couple_map_shift))
+    pair_rows = pairs(right, left, inverse, couple_map_matrix, row(couple_map_shift), size)
     return (after, pair_rows)
 
 

time: 97.3 us -> 88 us (0.904)
  Pallas kernels: 96.5 us -> 85.2 us
  local copies, waits for them, and re-layouts: 0 us -> 1.87 us
    pallas_call x2 -> x1, Pallas kernels: 49.3 us -> 37.8 us  [pairs(): pl.pallas_call(functools.partial(pair_kernel, size), in_specs=[hbm, hbm,...]
    unnamed x0 -> x1, local copies, waits for them, and re-layouts: none -> 1.87 us
where the time goes in v3:
time: 88 us; the launch traced here: 87.8 us
  Pallas kernels  85.2 us (97%)
  local copies, waits for them, and re-layouts  1.87 us (2%)
    pallas_call x1, Pallas kernels, pairs(): pl.pallas_call(functools.partial(pair_kernel, size), in_specs=[hbm, hbm,...  37.8 us
    pallas_call x1, Pallas kernels, exchange(): pl.pallas_call(functools.partial(exchange_kernel, size), out_shape=jax.Sh...  36.4 us
    pallas_call x1, Pallas kernels, attend(): pl.pallas_call(attend_kernel, out_shape=(jax.ShapeDtypeStruct((seqs, site...  11 us
    unnamed x1, local copies, waits for them, and re-layouts  1.87 us

profile of v3, /device:TPU:513, one launch (start us, length us, event | category | flops | bytes accessed | tf_op | source)
XLA Modules:
  0.0 87.8 jit_solution(1573389375786453991)
XLA Ops:
  0.6 36.4 %exchange.1 = bf16[2,64,2,8,256]{4,3,2,1,0:T(8,128)(2,1)} custom-call(bf16[2,64,8,256]{3,2,1,0:T(8,128)(2,1)} %bitcast.14), custom_call_target="tpu_custom_call" | custom-call | tf_op jit(solution)/shard_map/exchange/pallas_call | solution.py:492
  37.1 11.0 %attend.1 = (bf16[256,4,256]{2,1,0:T(4,128)(2,1)}, bf16[256,128]{1,0:T(8,128)(2,1)}, bf16[128,256]{1,0:T(8,128)(2,1)}, f32[512,128]{1,0:T(8,128)}) custom-call(s32[1]{0:T(128)} %bitcast.place_ref, bf16[2048,256]{1,0:T(8,128)(2,1)} %bitcast.13, s32[256,512]{1,0:T(8,128)} %present_ref.1, s32[1,256]{1,0:T(1,128)} %bitcast.16, f32[1,256]{1,0:T(1,128)} %bitcast.17, ...), custom_call_target="tpu_custom_call" | custom-call | tf_op jit(solution)/shard_map/attend/pallas_call | solution.py:175
  48.1 37.8 %pairs.1 = bf16[4,512,128]{2,1,0:T(8,128)(2,1)} custom-call(bf16[128,256]{1,0:T(8,128)(2,1)} %get-tuple-element.7.own_ref, bf16[256,128]{1,0:T(8,128)(2,1)} %get-tuple-element.8.left_ref, f32[512,128]{1,0:T(8,128)} %get-tuple-element.9.inverse_ref, bf16[1024,128]{1,0:T(8,128)(2,1)} %couple_ref.1, f32[1,128]{1,0:T(1,128)} %bitcast.24), custom_call_target="tpu_custom_call" | custom-call | tf_op jit(solution)/shard_map/pairs/pallas_call | solution.py:418
  85.9 1.9 %copy.19 = bf16[4,512,128]{2,1,0:T(8,128)(2,1)} copy(bf16[4,512,128]{2,1,0:T(8,128)(2,1)} %pairs.1) | data formatting | bytes 1048576

commit v4 on v2

--- a/solution.py
+++ b/solution.py
@@ -39,26 +39,51 @@
     return jnp.where(test(row, column), 1.0, 0.0)
 
 
-def attend_kernel(
-    place_ref, x_ref, present_ref, chain_ref, gain_ref, offset_ref, qk_ref, vg_ref, gate_ref,
-    exit_ref, exit_add_ref, gain2_ref, offset2_ref, twin_ref, shift_ref,
-    after_ref, left_ref, right_ref, inverse_ref,
-    xs, ys, keep, left_sum, right_sum,
+def core_kernel(
+    size, x_ref, present_ref, chain_ref, gain_ref, offset_ref, qk_ref, vg_ref, gate_ref,
+    exit_ref, exit_add_ref, gain2_ref, offset2_ref, twin_ref, shift_ref, couple_ref,
+    pair_shift_ref,
+    after_ref, out_ref,
+    xs, ys, keep, inverse, chunks, columns, blocks, wide, sums, terms, total, stage, placed,
+    main_recv, side_recv, swap_recv, out_recv, sends, local_sem,
 ):
     sites, seqs, width = xs.shape
     residues = present_ref.shape[1]
     pack = sites * OUTER_CHANNELS
     inner = HEAD_COUNT * HEAD_CHANNELS
-    place = place_ref[0]
-    core = lax.rem(place, 2)
-    blocks = x_ref.shape[0] // (2 * sites * OUTER_CHANNELS)
-    span = seqs // blocks
-
+    channels = 2 * OUTER_CHANNELS
+    chip_rows = 2 * sites
+    far = size // 2
+    mesh = pl.DeviceIdType.MESH
+    y, x, core = (lax.axis_index(a) for a in DAP)
+    main = jnp.where(core == 0, x, y)
+    side = jnp.where(core == 0, y, x)
+
+    def chip(first, second):
+        first, second = lax.rem(first + size, size), lax.rem(second + size, size)
+        return jnp.where(core == 0, second * size + first, first * size + second)
+
+    def device(first, second):
+        first, second = lax.rem(first + size, size), lax.rem(second + size, size)
+        return {
+            "dap_0": jnp.where(core == 0, second, first),
+            "dap_1": jnp.where(core == 0, first, second),
+        }
+
+    partner = {"dap_2": 1 - core}
+    barrier = pltpu.get_barrier_semaphore()
+    neighbours = [device(main + k, side) for k in range(1, size)]
+    neighbours += [device(main, side + k) for k in (1, -1, 2, -2)] + [partner]
+    for neighbour in neighbours:
+        pl.semaphore_signal(barrier, inc=1, device_id=neighbour, device_id_type=mesh)
+
+    groups = x_ref.shape[0] // (2 * sites * OUTER_CHANNELS)
+    span = seqs // groups
     pick = one_hot(
         sites * span, 2 * sites * span,
         lambda o, k: k == (o % span) * (2 * sites) + core * sites + o // span,
     ).astype(BF16)
-    for b in range(blocks):
+    for b in range(groups):
         rows = jnp.dot(
             pick, x_ref[2 * sites * span * b : 2 * sites * span * (b + 1), :],
             preferred_element_type=F32,
@@ -72,24 +97,79 @@
         lambda o, k: k == ((o % half) // 2) * 4 + (o // half) * 2 + o % 2,
     )
     order = (order * chain_ref[...].astype(F32)).astype(BF16)
-    present = present_ref[...].astype(F32)
-    live = jnp.dot(order, present.astype(BF16), preferred_element_type=F32).astype(BF16)
-    select = one_hot(
-        residues, pack, lambda j, c: j == place * sites + c // OUTER_CHANNELS
-    ).astype(BF16)
-    select_t = one_hot(
-        pack, residues, lambda c, j: j == place * sites + c % sites
-    ).astype(BF16)
-    live_l = jnp.dot(live, select, preferred_element_type=F32)
-    live_r = contract_lanes(select_t, live)
-    keep[...] = live_r[:8]
-    live_t = contract_lanes(present.T.astype(BF16), order).astype(BF16)
-    counts = jnp.dot(live_t, live_l.astype(BF16), preferred_element_type=F32)
-    inverse_ref[...] = 1.0 / jnp.maximum(counts, 1.0)
+    present = present_ref[...].astype(F32).astype(BF16)
+    live = jnp.dot(order, present, preferred_element_type=F32).astype(BF16)
+    own_site = (chip(main, side) * 2 + core) * sites
+    select = one_hot(8, residues, lambda o, j: j == own_site + o).astype(BF16)
+    keep[...] = contract_lanes(select, live)
 
     head_of_lane = lax.broadcasted_iota(jnp.int32, (1, inner), 1) // HEAD_CHANNELS
-    left_sum[...] = jnp.zeros_like(left_sum)
-    right_sum[...] = jnp.zeros_like(right_sum)
+    shift = jnp.sum(
+        one_hot(channels, channels, lambda o, c: o == c) * shift_ref[...], axis=1, keepdims=True
+    )
+
+    def remote(src, dst, send, recv, target):
+        return pltpu.make_async_remote_copy(
+            src_ref=src, dst_ref=dst, send_sem=sends.at[send], recv_sem=recv,
+            device_id=target, device_id_type=mesh,
+        )
+
+    def index(offset):
+        return offset % size
+
+    def ring(r, along_main, origin, sign, step):
+        reach = origin - sign * step
+        if along_main:
+            ref = lambda offset: chunks.at[index(offset), r]
+            target, recv, send = device(main + sign * step, side), main_recv, 0
+        else:
+            ref = lambda offset: columns.at[index(offset), core, r]
+            target, recv, send = device(main, side + sign * step), side_recv, 1
+        src, dst = ref(origin), ref(reach)
+        where = index(reach)
+        if abs(reach) == far:
+            rows = (channels if along_main else OUTER_CHANNELS) // 2
+            first = 0 if sign > 0 else rows
+            src, dst = src.at[pl.ds(first, rows)], dst.at[pl.ds(first, rows)]
+            where = far if sign > 0 else size
+        return remote(src, dst, send, recv.at[r, where], target)
+
+    def swap(r, offset):
+        return remote(
+            chunks.at[index(offset), r, pl.ds(OUTER_CHANNELS, OUTER_CHANNELS)],
+            columns.at[index(offset), core, r], 2, swap_recv.at[r, index(offset)], partner,
+        )
+
+    def swap_wait(r, offset):
+        ref = columns.at[index(offset), 1 - core, r]
+        remote(ref, ref, 2, swap_recv.at[r, index(offset)], partner).wait_recv()
+
+    def launch(r):
+        for step in (2, 1):
+            for along_main in (True, False):
+                for sign in (1, -1):
+                    ring(r, along_main, 0, sign, step).start()
+        swap(r, 0).start()
+
+    def relay(r):
+        for along_main in (True, False):
+            for sign in (1, -1):
+                ring(r, along_main, 0, sign, 2).wait_recv()
+                ring(r, along_main, -2 * sign, sign, 2).start()
+                ring(r, along_main, -2 * sign, sign, 1).start()
+                if along_main:
+                    swap(r, -2 * sign).start()
+        for sign in (1, -1):
+            ring(r, True, 0, sign, 1).wait_recv()
+            swap(r, -sign).start()
+
+    def relay_far(r):
+        for sign in (1, -1):
+            ring(r, True, -2 * sign, sign, 1).wait_recv()
+            swap(r, -3 * sign).start()
+        for sign in (1, -1):
+            ring(r, True, -2 * sign, sign, 2).wait_recv()
+        swap(r, far).start()
 
     def one_site(r, carry):
         x = xs[r].astype(F32)
@@ -100,48 +180,39 @@
         key = query_key[:, inner:].astype(BF16)
         value = value_gate[:, :inner].astype(BF16)
         gate = jax.nn.sigmoid(value_gate[:, inner:] + gate_ref[...])
-        alive = keep[pl.ds(r, 1), :] > 0
+        present_row = keep[pl.ds(r, 1), :]
+        alive = present_row > 0
         mixed = jnp.zeros((seqs, inner), F32)
         for h in range(HEAD_COUNT):
             own = head_of_lane == h
             query_h = query * own.astype(F32).astype(BF16)
             scores = jnp.where(alive, contract_lanes(query_h, key), MASKED)
             exponent = jnp.exp(scores - jnp.max(scores, axis=-1, keepdims=True))
-            total = jnp.sum(exponent, axis=-1, keepdims=True)
+            weight = jnp.sum(exponent, axis=-1, keepdims=True)
             part = jnp.dot(exponent.astype(BF16), value, preferred_element_type=F32)
-            mixed = jnp.where(own, part * (1.0 / total), mixed)
+            mixed = jnp.where(own, part * (1.0 / weight), mixed)
         gated = (mixed * gate).astype(BF16)
         update = jnp.dot(gated, exit_ref[...], preferred_element_type=F32) + exit_add_ref[...]
         after = (x + update).astype(BF16)
+        again = normalize(after.astype(F32), gain2_ref[...], offset2_ref[...])
+        both = ((contract_lanes(twin_ref[...], again) + shift) * present_row).astype(BF16)
+        chunks[0, r] = both
+        columns[0, core, r] = both[OUTER_CHANNELS:]
         ys[r] = after
-        again = normalize(after.astype(F32), gain2_ref[...], offset2_ref[...])
-        channels = 2 * OUTER_CHANNELS
-        spread_l = one_hot(
-            pack, channels,
-            lambda o, c: (c == o % OUTER_CHANNELS) & (o // OUTER_CHANNELS == r),
-        ).astype(BF16)
-        spread_r = one_hot(
-            pack, channels,
-            lambda o, c: (c == OUTER_CHANNELS + o // sites) & (o % sites == r),
-        ).astype(BF16)
-        twin_l = jnp.dot(spread_l, twin_ref[...], preferred_element_type=F32).astype(BF16)
-        twin_r = jnp.dot(spread_r, twin_ref[...], preferred_element_type=F32).astype(BF16)
-        left_sum[...] += contract_lanes(again, twin_l)
-        right_sum[...] += contract_lanes(twin_r, again)
+
+        @pl.when(r == 0)
+        def _():
+            pl.semaphore_wait(barrier, len(neighbours))
+
+        launch(r)
+
+        @pl.when(r >= 2)
+        def _():
+            relay(r - 2)
+
         return carry
 
     lax.fori_loop(0, sites, one_site, 0)
-    channels = 2 * OUTER_CHANNELS
-    shift = shift_ref[...]
-    across = one_hot(pack, channels, lambda o, c: c == OUTER_CHANNELS + o // sites)
-    shift_r = jnp.sum(across * shift, axis=1, keepdims=True)
-    column = jnp.sum(
-        one_hot(channels, channels, lambda a, c: a == c) * shift, axis=1, keepdims=True
-    )
-    down = one_hot(channels, pack, lambda c, o: c == o % OUTER_CHANNELS)
-    shift_l = jnp.sum(down * column, axis=0, keepdims=True)
-    left_ref[...] = ((left_sum[...] + shift_l) * live_l).astype(BF16)
-    right_ref[...] = ((right_sum[...] + shift_r) * live_r).astype(BF16)
 
     group = 2 * span
     place_back = one_hot(
@@ -163,114 +234,184 @@
             axis=0,
         )
         rows = jnp.dot(place_back, stack, preferred_element_type=F32).astype(BF16)
-        after_ref[group * g : group * (g + 1)] = rows.reshape(group, sites, width)
-
-
-def attend(place, x, present, *rest):
+        placed[group * g : group * (g + 1)] = rows.reshape(group, sites, width)
+
+    wide[...] = couple_ref[...].astype(F32)
+    blocks[...] = jnp.zeros_like(blocks)
+    for e in range(OUTER_CHANNELS):
+        rows = wide[pl.ds(e, OUTER_CHANNELS, stride=OUTER_CHANNELS), :].astype(BF16)
+        for i in range(sites):
+            row = e * pack + i * OUTER_CHANNELS
+            blocks[row : row + OUTER_CHANNELS, i * PAIR_DIM : (i + 1) * PAIR_DIM] = rows
+    relay(sites - 2)
+
+    def row_site(k):
+        first = lax.rem(main + k // sites, size)
+        at = jnp.where(core == 0, side * size + first, first * size + side)
+        return (at * 2 + core) * sites + k % sites
+
+    def column_site(k):
+        second = lax.rem(side + k // chip_rows, size)
+        at = jnp.where(core == 0, second * size + main, main * size + second)
+        return at * chip_rows + k % chip_rows
+
+    lanes = size * sites
+    row_pick = one_hot(
+        residues, 128, lambda j, k: (j == row_site(k)) & (k < lanes)
+    ).astype(BF16)
+    column_pick = one_hot(size * chip_rows, residues, lambda k, j: j == column_site(k)).astype(BF16)
+    live_rows = jnp.dot(live, row_pick, preferred_element_type=F32).astype(BF16)
+    live_columns = contract_lanes(column_pick, live).astype(BF16)
+    counts = jnp.dot(live_columns, live_rows, preferred_element_type=F32).astype(BF16)
+    spread = one_hot(128, size * pack, lambda k, l: k == l // OUTER_CHANNELS).astype(BF16)
+    counts = jnp.dot(counts, spread, preferred_element_type=F32)
+    inverse[...] = 1.0 / jnp.maximum(counts, 1.0)
+
+    after_copy = pltpu.make_async_copy(placed, after_ref, local_sem.at[0])
+    after_copy.start()
+    relay(sites - 1)
+
+    near = [0, -1, 1, -2, 2]
+    quads = [(-2, 2), (-1, 1), (0, -3), (3, far)]
+    batches = [[far, -3, 3, 2], [0, -1, 1, -2]]
+    ranks = batches[0] + batches[1]
+    turn = [0]
+
+    def multiply(offset, q):
+        members = [index(b) for b in quads[q]]
+        quad = jnp.concatenate(
+            [columns[b].reshape(chip_rows * OUTER_CHANNELS, seqs) for b in members], axis=0
+        )
+        left = chunks[index(offset), :, :OUTER_CHANNELS, :].reshape(pack, seqs)
+        buffer = turn[0] % 2
+        turn[0] += 1
+        sums[buffer] = contract_lanes(quad, left)
+        lanes = slice(pack * index(offset), pack * (index(offset) + 1))
+        scale = jnp.concatenate(
+            [inverse[chip_rows * b : chip_rows * (b + 1), lanes] for b in members], axis=0
+        )
+        first = ranks.index(offset) * size * chip_rows + 2 * chip_rows * q
+        for e in range(OUTER_CHANNELS):
+            rows = sums[buffer, pl.ds(e, 2 * chip_rows, stride=OUTER_CHANNELS), :]
+            terms[first : first + 2 * chip_rows, e * pack : (e + 1) * pack] = (
+                rows * scale
+            ).astype(BF16)
+
+    def project(batch):
+        count = size * chip_rows
+        first = batch * len(batches[0]) * count
+        rows = slice(first, first + len(batches[0]) * count)
+        result = jnp.dot(terms[rows, :], blocks[...], preferred_element_type=F32)
+        for k in range(len(batches[0])):
+            for q, members in enumerate(quads):
+                for t, b in enumerate(members):
+                    row = k * count + (2 * q + t) * chip_rows
+                    to = lax.rem(side + b + size, size) * chip_rows
+                    to = pl.multiple_of(first + k * count + to, chip_rows)
+                    total[pl.ds(to, chip_rows), :] = result[row : row + chip_rows]
+        for k in range(len(batches[0])):
+            at = batch * len(batches[0]) + k
+            for i in range(sites):
+                part = total[at * count : (at + 1) * count, i * PAIR_DIM : (i + 1) * PAIR_DIM]
+                part = (part + pair_shift_ref[...]).astype(BF16)
+                stage[at, i] = part.reshape(size, chip_rows, PAIR_DIM)
+
+    def deliver(batch):
+        for offset in batches[batch]:
+            src = stage.at[ranks.index(offset)]
+            for c in range(2):
+
+                @pl.when(core == c)
+                def _():
+                    dst = out_ref.at[:, :, main] if c == 0 else out_ref.at[:, main]
+                    if offset:
+                        remote(src, dst, 3, out_recv, device(main + offset, side)).start()
+                    else:
+                        pltpu.make_async_copy(src, dst, local_sem.at[1]).start()
+
+    for r in range(sites):
+        for sign in (1, -1):
+            ring(r, False, 0, sign, 1).wait_recv()
+        for offset in near:
+            swap_wait(r, offset)
+    for q in (0, 1):
+        for offset in near:
+            multiply(offset, q)
+    for r in range(sites):
+        relay_far(r)
+    for r in range(sites):
+        for step in (1, 2):
+            for sign in (1, -1):
+                ring(r, False, -2 * sign, sign, step).wait_recv()
+        for offset in (-3, 3, far):
+            swap_wait(r, offset)
+    for batch in (0, 1):
+        for offset in batches[batch]:
+            for q in range(len(quads)):
+                if q > 1 or offset not in near:
+                    multiply(offset, q)
+        project(batch)
+        deliver(batch)
+
+    for buffer, send in (
+        (chunks.at[pl.ds(0, size - 1)], 0),
+        (columns.at[pl.ds(0, size - 1), 0], 1),
+        (columns.at[:, 0], 2),
+        (stage.at[pl.ds(0, size - 1)], 3),
+    ):
+        pltpu.make_async_copy(buffer, buffer, sends.at[send]).wait()
+    arrived = stage.at[pl.ds(0, size - 1)]
+    pltpu.make_async_copy(arrived, arrived, out_recv).wait()
+    own = stage.at[ranks.index(0)]
+    pltpu.make_async_copy(own, own, local_sem.at[1]).wait()
+    after_copy.wait()
+
+
+def attend_pairs(x, present, *rest, size):
     seqs, residues = present.shape
     width = x.shape[1]
     sites = x.shape[0] // (2 * seqs)
     pack = sites * OUTER_CHANNELS
+    chip_rows = 2 * sites
+    couple = rest[-2]
+    count = size * chip_rows
+    hbm = pl.BlockSpec(memory_space=pl.ANY)
     vmem = pl.BlockSpec(memory_space=pltpu.VMEM)
+    dma = pltpu.SemaphoreType.DMA
     return pl.pallas_call(
-        attend_kernel,
+        functools.partial(core_kernel, size),
         out_shape=(
             jax.ShapeDtypeStruct((seqs, sites, width), BF16),
-            jax.ShapeDtypeStruct((seqs, pack), BF16),
-            jax.ShapeDtypeStruct((pack, seqs), BF16),
-            jax.ShapeDtypeStruct((residues, pack), F32),
+            jax.ShapeDtypeStruct((sites, size, size, chip_rows, PAIR_DIM), BF16),
         ),
-        in_specs=[pl.BlockSpec(memory_space=pltpu.SMEM)] + [vmem] * (2 + len(rest)),
-        out_specs=(vmem,) * 4,
+        in_specs=[vmem] * (2 + len(rest)),
+        out_specs=(hbm, hbm),
         scratch_shapes=[
             pltpu.VMEM((sites, seqs, width), BF16),
             pltpu.VMEM((sites, seqs, width), BF16),
             pltpu.VMEM((8, seqs), F32),
-            pltpu.VMEM((seqs, pack), F32),
-            pltpu.VMEM((pack, seqs), F32),
-        ],
-        compiler_params=pltpu.CompilerParams(vmem_limit_bytes=VMEM_LIMIT),
-        name="attend",
-    )(place, x, present, *rest)
-
-
-def pair_kernel(right_ref, left_ref, inverse_ref, couple_ref, shift_ref, out_ref, terms, blocks, wide):
-    step = pl.program_id(0)
-    owners, pack, seqs = right_ref.shape
-    sites = out_ref.shape[0]
-    chip_rows = 2 * sites
-    halves = OUTER_CHANNELS // 2
-
-    @pl.when(step == 0)
-    def _():
-        wide[...] = couple_ref[...].astype(F32)
-        blocks[...] = jnp.zeros_like(blocks)
-        for e in range(OUTER_CHANNELS):
-            part = wide[pl.ds(e, OUTER_CHANNELS, stride=OUTER_CHANNELS), :].astype(BF16)
-            for i in range(sites):
-                row = e * pack + i * OUTER_CHANNELS
-                blocks[row : row + OUTER_CHANNELS, i * PAIR_DIM : (i + 1) * PAIR_DIM] = part
-
-    lower = lax.broadcasted_iota(jnp.int32, (1, chip_rows, 1), 1) < sites
-    left = left_ref[...]
-
-    def four(u, carry):
-        quad = right_ref[pl.ds(4 * u, 4)].reshape(4 * pack, seqs)
-        sums = jnp.dot(quad, left, preferred_element_type=F32)
-        sums = sums.reshape(4, halves, chip_rows, pack)
-        even, odd = [], []
-        for t in range(2):
-            a, b = sums[2 * t], sums[2 * t + 1]
-            first = pl.multiple_of((step * owners + 4 * u + 2 * t) * sites, chip_rows)
-            scale = inverse_ref[pl.ds(first, chip_rows), :][None]
-            even.append(jnp.where(lower, a, pltpu.roll(b, sites, 1)) * scale)
-            odd.append(jnp.where(lower, pltpu.roll(a, sites, 1), b) * scale)
-        rows = pl.ds(pl.multiple_of((step * owners + 4 * u) * sites, 2 * chip_rows), 2 * chip_rows)
-        even = jnp.concatenate(even, axis=1).astype(BF16)
-        odd = jnp.concatenate(odd, axis=1).astype(BF16)
-        for e in range(halves):
-            terms[rows, 2 * e * pack : (2 * e + 1) * pack] = even[e]
-            terms[rows, (2 * e + 1) * pack : (2 * e + 2) * pack] = odd[e]
-        return carry
-
-    lax.fori_loop(0, owners // 4, four, 0)
-
-    @pl.when(step == pl.num_programs(0) - 1)
-    def _():
-        total = jnp.dot(terms[...], blocks[...], preferred_element_type=F32)
-        for i in range(sites):
-            part = total[:, i * PAIR_DIM : (i + 1) * PAIR_DIM] + shift_ref[...]
-            out_ref[i] = part.astype(BF16)
-
-
-def pairs(right_all, left, inverse, couple, shift):
-    owners, pack, seqs = right_all.shape
-    residues = inverse.shape[0]
-    sites = pack // OUTER_CHANNELS
-    steps = 4
-    whole = lambda *shape: pl.BlockSpec(shape, lambda g: (0,) * len(shape))
-    return pl.pallas_call(
-        pair_kernel,
-        grid=(steps,),
-        in_specs=[
-            pl.BlockSpec((owners // steps, pack, seqs), lambda g: (g, 0, 0)),
-            whole(*left.shape),
-            whole(*inverse.shape),
-            whole(*couple.shape),
-            whole(*shift.shape),
-        ],
-        out_specs=whole(sites, residues, PAIR_DIM),
-        out_shape=jax.ShapeDtypeStruct((sites, residues, PAIR_DIM), BF16),
-        scratch_shapes=[
-            pltpu.VMEM((residues, OUTER_CHANNELS * pack), BF16),
+            pltpu.VMEM((count, size * pack), F32),
+            pltpu.VMEM((size, sites, 2 * OUTER_CHANNELS, seqs), BF16),
+            pltpu.VMEM((size, 2, sites, OUTER_CHANNELS, seqs), BF16),
             pltpu.VMEM((OUTER_CHANNELS * pack, sites * PAIR_DIM), BF16),
             pltpu.VMEM(couple.shape, F32),
+            pltpu.VMEM((2, 2 * chip_rows * OUTER_CHANNELS, pack), F32),
+            pltpu.VMEM((size * count, OUTER_CHANNELS * pack), BF16),
+            pltpu.VMEM((size * count, sites * PAIR_DIM), F32),
+            pltpu.VMEM((size, sites, size, chip_rows, PAIR_DIM), BF16),
+            pltpu.VMEM((seqs, sites, width), BF16),
+            dma((sites, size + 1)),
+            dma((sites, size + 1)),
+            dma((sites, size)),
+            dma,
+            dma((4,)),
+            dma((2,)),
         ],
         compiler_params=pltpu.CompilerParams(
-            vmem_limit_bytes=VMEM_LIMIT, dimension_semantics=("arbitrary",)
+            vmem_limit_bytes=VMEM_LIMIT, collective_id=1, has_side_effects=True
         ),
-        name="pairs",
-    )(right_all, left, inverse, couple, shift)
+        name="attend_pairs",
+    )(x, present, *rest)
 
 
 def exchange_kernel(size, x_ref, out_ref, sent, got, swap_send, swap_got, own_sem):
@@ -510,8 +651,7 @@
     width = homolog_stack_tensor.shape[-1]
     size = lax.axis_size("dap_0")
     row = lambda v: v[None, :]
-    after, left, right, inverse = attend(
-        lax.axis_index(DAP)[None],
+    after, pair_rows = attend_pairs(
         exchange(homolog_stack_tensor, size),
         occupancy_indicator,
         row(chain_existence_flags),
@@ -526,10 +666,11 @@
         row(product_mean_layer_shift),
         twin_map_matrix.T,
         row(twin_map_shift),
+        couple_map_matrix,
+        row(couple_map_shift),
+        size=size,
     )
-    right_all = gather_right(right, size)
-    pair_rows = pairs(right_all, left, inverse, couple_map_matrix, row(couple_map_shift))
-    return (after, pair_rows)
+    return (after, pair_rows.reshape(-1, residues, PAIR_DIM))
 
 
 def solution(mesh):

time: 97.3 us -> 75.7 us (0.78)
  Pallas kernels: 96.5 us -> 72 us
  local copies, waits for them, and re-layouts: 0 us -> 2.87 us
    pallas_call x3 -> x1, Pallas kernels: 60.1 us -> 35.6 us  [attend_pairs(): pl.pallas_call(functools.partial(core_kernel, size), out_shape=(jax.Shape...]
    unnamed x0 -> x4, local copies, waits for them, and re-layouts: none -> 2.87 us
where the time goes in v4:
time: 75.7 us; the launch traced here: 75.6 us
  Pallas kernels  72 us (95%)
  local copies, waits for them, and re-layouts  2.87 us (4%)
    pallas_call x1, Pallas kernels, exchange(): pl.pallas_call(functools.partial(exchange_kernel, size), out_shape=jax.Sh...  36.4 us
    pallas_call x1, Pallas kernels, attend_pairs(): pl.pallas_call(functools.partial(core_kernel, size), out_shape=(jax.Shape...  35.6 us
    unnamed x4, local copies, waits for them, and re-layouts  2.87 us

profile of v4, /device:TPU:513, one launch (start us, length us, event | category | flops | bytes accessed | tf_op | source)
XLA Modules:
  0.0 75.6 jit_solution(11147794880250741229)
XLA Ops:
  0.6 36.4 %exchange.1 = bf16[2,64,2,8,256]{4,3,2,1,0:T(8,128)(2,1)} custom-call(bf16[2,64,8,256]{3,2,1,0:T(8,128)(2,1)} %bitcast.14), custom_call_target="tpu_custom_call" | custom-call | tf_op jit(solution)/shard_map/exchange/pallas_call | solution.py:464
  37.1 35.6 %attend_pairs.1 = (bf16[256,4,256]{2,1,0:T(4,128)(2,1)}, bf16[4,8,8,8,128]{4,3,2,1,0:T(8,128)(2,1)}) custom-call(bf16[2048,256]{1,0:T(8,128)(2,1)} %bitcast.13, s32[256,512]{1,0:T(8,128)} %present_ref.1, s32[1,256]{1,0:T(1,128)} %bitcast.17, f32[1,256]{1,0:T(1,128)} %bitcast.18, f32[1,256]{1,0:T(1,128)} %bitcast.19, bf16[256,512]{1,0:T(8,128)(2,1)} %qk_ref.1, ...), custom_call_target="tpu_custom_call" | custom-call | tf_op jit(solution)/shard_map/attend_pairs/pallas_call | solution.py:381
  72.7 0.0 copy-start
  72.7 2.1 %copy.20 = bf16[256,4,256]{2,1,0:T(4,128)(2,1)} copy(bf16[256,4,256]{2,1,0:T(4,128)(2,1)} %get-tuple-element.8) | data formatting | bytes 1048576
  74.8 0.0 copy-done
  74.8 0.8 %copy.21 = bf16[4,512,128]{2,1,0:T(8,128)(2,1)} copy(bf16[4,512,128]{2,1,0:T(8,128)(2,1)S(1)} %bitcast.15) | data formatting | bytes 1048576
Async XLA Ops:
  72.7 2.1 %copy-start = (bf16[4,8,8,8,128]{4,3,2,1,0:T(8,128)(2,1)S(1)}, bf16[4,8,8,8,128]{4,3,2,1,0:T(8,128)(2,1)}, u32[]{:S(2)}) copy-start(bf16[4,8,8,8,128]{4,3,2,1,0:T(8,128)(2,1)} %get-tuple-element.5) | copy-start | bytes 1572868

commit v5 on v4

v5 whole, which is shorter than its diff:
```python
import functools

import jax
import jax.numpy as jnp
from jax import lax
from jax.experimental import pallas as pl
from jax.experimental.pallas import tpu as pltpu
from jax.sharding import Mesh
from jax.sharding import PartitionSpec as P

HEAD_COUNT = 8
HEAD_CHANNELS = 32
OUTER_CHANNELS = 32
PAIR_DIM = 128
DAP = ("dap_0", "dap_1", "dap_2")
GRP_DAP = ("grp", "dap_0", "dap_1", "dap_2")
F32 = jnp.float32
BF16 = jnp.bfloat16
VMEM_LIMIT = 60 * 1024 * 1024
PITCH = 40


EPSILON = 1e-05
MASKED = -100000.0


def normalize(widened, gain, offset):
    centred = widened - jnp.mean(widened, axis=-1, keepdims=True)
    variance = jnp.mean(centred * centred, axis=-1, keepdims=True)
    return (centred * lax.rsqrt(variance + EPSILON) * gain + offset).astype(BF16)


def contract_lanes(a, b):
    return lax.dot_general(a, b, (((1,), (1,)), ((), ())), preferred_element_type=F32)


def one_hot(rows, columns, test):
    row = lax.broadcasted_iota(jnp.int32, (rows, columns), 0)
    column = lax.broadcasted_iota(jnp.int32, (rows, columns), 1)
    return jnp.where(test(row, column), 1.0, 0.0)


def core_kernel(
    size, source_ref, present_hbm, qk_hbm, vg_hbm, exit_hbm, couple_hbm, chain_ref, gain_ref,
    offset_ref, gate_ref, exit_add_ref, gain2_ref, offset2_ref, twin_ref, shift_ref,
    pair_shift_ref,
    after_ref, out_ref,
    landed, present_ref, qk_ref, vg_ref, exit_ref, couple_ref, xs, ys, keep, inverse, chunks, columns, blocks, wide, sums, terms, total, stage, placed,
    main_recv, side_recv, swap_recv, out_recv, sends, local_sem, load_sem, got, sent, crossed,
):
    sites, seqs, width = xs.shape
    residues = present_ref.shape[1]
    pack = sites * OUTER_CHANNELS
    inner = HEAD_COUNT * HEAD_CHANNELS
    channels = 2 * OUTER_CHANNELS
    chip_rows = 2 * sites
    far = size // 2
    mesh = pl.DeviceIdType.MESH
    y, x, core = (lax.axis_index(a) for a in DAP)
    main = jnp.where(core == 0, x, y)
    side = jnp.where(core == 0, y, x)

    def chip(first, second):
        first, second = lax.rem(first + size, size), lax.rem(second + size, size)
        return jnp.where(core == 0, second * size + first, first * size + second)

    def device(first, second):
        first, second = lax.rem(first + size, size), lax.rem(second + size, size)
        return {
            "dap_0": jnp.where(core == 0, second, first),
            "dap_1": jnp.where(core == 0, first, second),
        }

    partner = {"dap_2": 1 - core}
    chips = size * size
    here = y * size + x
    away = lambda d: min(d, size - d)
    steps = [(dy, dx) for dy in range(size) for dx in range(size) if dy or dx]
    steps.sort(key=lambda d: -(away(d[0]) + away(d[1])))
    barrier = pltpu.get_barrier_semaphore()
    for dy, dx in steps:
        peer = {"dap_0": lax.rem(y + dy, size), "dap_1": lax.rem(x + dx, size)}
        pl.semaphore_signal(barrier, inc=1, device_id=peer, device_id_type=mesh)
    pl.semaphore_signal(barrier, inc=1, device_id=partner, device_id_type=mesh)
    own_rows = pltpu.make_async_copy(
        source_ref.at[:, here], landed.at[core, here], local_sem.at[2]
    )
    own_rows.start()
    loads = [
        pltpu.make_async_copy(a, b, load_sem.at[i])
        for i, (a, b) in enumerate(
            (
                (present_hbm, present_ref),
                (couple_hbm, couple_ref),
                (qk_hbm, qk_ref),
                (vg_hbm, vg_ref),
                (exit_hbm, exit_ref),
            )
        )
    ]
    for load in loads:
        load.start()
    pl.semaphore_wait(barrier, chips)
    for dy, dx in steps:
        row, column = lax.rem(y + dy, size), lax.rem(x + dx, size)
        pltpu.make_async_remote_copy(
            src_ref=source_ref.at[:, row * size + column], dst_ref=landed.at[core, here],
            send_sem=sent, recv_sem=got, device_id={"dap_0": row, "dap_1": column},
            device_id_type=mesh,
        ).start()
    for load in loads:
        load.wait()

    half = seqs // 2
    order = one_hot(
        seqs, seqs,
        lambda o, k: k == ((o % half) // 2) * 4 + (o // half) * 2 + o % 2,
    )
    order = (order * chain_ref[...].astype(F32)).astype(BF16)
    present = present_ref[...].astype(F32).astype(BF16)
    live = jnp.dot(order, present, preferred_element_type=F32).astype(BF16)
    own_site = (chip(main, side) * 2 + core) * sites
    select = one_hot(8, residues, lambda o, j: j == own_site + o).astype(BF16)
    keep[...] = contract_lanes(select, live)

    head_of_lane = lax.broadcasted_iota(jnp.int32, (1, inner), 1) // HEAD_CHANNELS
    shift = jnp.sum(
        one_hot(channels, channels, lambda o, c: o == c) * shift_ref[...], axis=1, keepdims=True
    )

    wide[...] = couple_ref[...].astype(F32)
    blocks[...] = jnp.zeros_like(blocks)
    for e in range(OUTER_CHANNELS):
        rows = wide[pl.ds(e, OUTER_CHANNELS, stride=OUTER_CHANNELS), :].astype(BF16)
        for i in range(sites):
            row = e * pack + i * OUTER_CHANNELS
            blocks[row : row + OUTER_CHANNELS, i * PAIR_DIM : (i + 1) * PAIR_DIM] = rows
    def row_site(k):
        first = lax.rem(main + k // sites, size)
        at = jnp.where(core == 0, side * size + first, first * size + side)
        return (at * 2 + core) * sites + k % sites

    def column_site(k):
        second = lax.rem(side + k // chip_rows, size)
        at = jnp.where(core == 0, second * size + main, main * size + second)
        return at * chip_rows + k % chip_rows

    lanes = size * sites
    row_pick = one_hot(
        residues, 128, lambda j, k: (j == row_site(k)) & (k < lanes)
    ).astype(BF16)
    column_pick = one_hot(size * chip_rows, residues, lambda k, j: j == column_site(k)).astype(BF16)
    live_rows = jnp.dot(live, row_pick, preferred_element_type=F32).astype(BF16)
    live_columns = contract_lanes(column_pick, live).astype(BF16)
    counts = jnp.dot(live_columns, live_rows, preferred_element_type=F32).astype(BF16)
    spread = one_hot(128, size * pack, lambda k, l: k == l // OUTER_CHANNELS).astype(BF16)
    counts = jnp.dot(counts, spread, preferred_element_type=F32)
    inverse[...] = 1.0 / jnp.maximum(counts, 1.0)

    others = landed.at[core, pl.ds(0, chips - 1)]
    own_rows.wait()
    pltpu.make_async_copy(others, others, got).wait()
    cross = pltpu.make_async_remote_copy(
        src_ref=landed.at[core], dst_ref=landed.at[core], send_sem=crossed.at[0],
        recv_sem=crossed.at[1], device_id=partner, device_id_type=mesh,
    )
    cross.start()

    span = OUTER_CHANNELS
    pick = one_hot(
        sites * span, 2 * sites * span,
        lambda o, k: k == (o % span) * (2 * sites) + core * sites + o // span,
    ).astype(BF16)
    band = 2 * sites * span

    def sort_rows(which):
        rows_in = landed[which].reshape(chips * 2 * 2 * sites, width)
        for b in range(half // span):
            rows = jnp.dot(
                pick, rows_in[band * b : band * (b + 1)], preferred_element_type=F32
            ).astype(BF16)
            for r in range(sites):
                first = pl.multiple_of(which * half + span * b, span)
                xs[r, pl.ds(first, span), :] = rows[span * r : span * (r + 1)]

    sort_rows(core)
    pltpu.make_async_copy(others, others, sent).wait()
    cross.wait()
    sort_rows(1 - core)

    def remote(src, dst, send, recv, target):
        return pltpu.make_async_remote_copy(
            src_ref=src, dst_ref=dst, send_sem=sends.at[send], recv_sem=recv,
            device_id=target, device_id_type=mesh,
        )

    def index(offset):
        return offset % size

    def ring(r, along_main, origin, sign, step, whole=False):
        reach = origin - sign * step
        if along_main:
            ref = lambda offset: chunks.at[index(offset), r]
            target, recv, send = device(main + sign * step, side), main_recv, 0
        else:
            ref = lambda offset: columns.at[index(offset), core, r]
            target, recv, send = device(main, side + sign * step), side_recv, 1
        src, dst = ref(origin), ref(reach)
        where = index(reach)
        if abs(reach) == far and not whole:
            rows = (channels if along_main else OUTER_CHANNELS) // 2
            first = 0 if sign > 0 else rows
            src, dst = src.at[pl.ds(first, rows)], dst.at[pl.ds(first, rows)]
            where = far if sign > 0 else size
        return remote(src, dst, send, recv.at[r, where], target)

    def swap(r, offset):
        return remote(
            chunks.at[index(offset), r, pl.ds(OUTER_CHANNELS, OUTER_CHANNELS)],
            columns.at[index(offset), core, r], 2, swap_recv.at[r, index(offset)], partner,
        )

    def swap_wait(r, offset):
        ref = columns.at[index(offset), 1 - core, r]
        remote(ref, ref, 2, swap_recv.at[r, index(offset)], partner).wait_recv()

    def launch(r):
        for step in (2, 1):
            for along_main in (True, False):
                for sign in (1, -1):
                    ring(r, along_main, 0, sign, step).start()
        swap(r, 0).start()

    def launch_all(r):
        for step in (far, 3, 2, 1):
            for along_main in (True, False):
                for sign in (1, -1) if step < far else (1,):
                    ring(r, along_main, 0, sign, step, True).start()
        swap(r, 0).start()

    def relay_all(r):
        for step in (1, 2, 3, far):
            for sign in (1, -1) if step < far else (1,):
                ring(r, True, 0, sign, step, True).wait_recv()
                swap(r, index(-sign * step)).start()

    def relay(r):
        for along_main in (True, False):
            for sign in (1, -1):
                ring(r, along_main, 0, sign, 2).wait_recv()
                ring(r, along_main, -2 * sign, sign, 2).start()
                ring(r, along_main, -2 * sign, sign, 1).start()
                if along_main:
                    swap(r, -2 * sign).start()
        for sign in (1, -1):
            ring(r, True, 0, sign, 1).wait_recv()
            swap(r, -sign).start()

    def relay_far(r):
        for sign in (1, -1):
            ring(r, True, -2 * sign, sign, 1).wait_recv()
            swap(r, -3 * sign).start()
        for sign in (1, -1):
            ring(r, True, -2 * sign, sign, 2).wait_recv()
        swap(r, far).start()

    def one_site(r, carry):
        x = xs[r].astype(F32)
        normed = normalize(x, gain_ref[...], offset_ref[...])
        query_key = jnp.dot(normed, qk_ref[...], preferred_element_type=F32)
        value_gate = jnp.dot(normed, vg_ref[...], preferred_element_type=F32)
        query = (query_key[:, :inner] * HEAD_CHANNELS ** (-0.5)).astype(BF16)
        key = query_key[:, inner:].astype(BF16)
        value = value_gate[:, :inner].astype(BF16)
        gate = jax.nn.sigmoid(value_gate[:, inner:] + gate_ref[...])
        present_row = keep[pl.ds(r, 1), :]
        alive = present_row > 0
        mixed = jnp.zeros((seqs, inner), F32)
        for h in range(HEAD_COUNT):
            own = head_of_lane == h
            query_h = query * own.astype(F32).astype(BF16)
            scores = jnp.where(alive, contract_lanes(query_h, key), MASKED)
            exponent = jnp.exp(scores - jnp.max(scores, axis=-1, keepdims=True))
            weight = jnp.sum(exponent, axis=-1, keepdims=True)
            part = jnp.dot(exponent.astype(BF16), value, preferred_element_type=F32)
            mixed = jnp.where(own, part * (1.0 / weight), mixed)
        gated = (mixed * gate).astype(BF16)
        update = jnp.dot(gated, exit_ref[...], preferred_element_type=F32) + exit_add_ref[...]
        after = (x + update).astype(BF16)
        again = normalize(after.astype(F32), gain2_ref[...], offset2_ref[...])
        both = ((contract_lanes(twin_ref[...], again) + shift) * present_row).astype(BF16)
        chunks[0, r] = both
        columns[0, core, r] = both[OUTER_CHANNELS:]
        ys[r] = after

        @pl.when(r < sites - 1)
        def _():
            launch(r)

        @pl.when(r == sites - 1)
        def _():
            launch_all(r)

        @pl.when(r >= 2)
        def _():
            relay(r - 2)

        return carry

    lax.fori_loop(0, sites, one_site, 0)

    group = 2 * span
    place_back = one_hot(
        group * sites, group * sites,
        lambda o, k: k
        == (
            ((o % sites) * 2 + (o // (2 * sites)) % 2) * span
            + (o // (4 * sites)) * 2
            + (o // sites) % 2
        ),
    ).astype(BF16)
    for g in range(seqs // group):
        stack = jnp.concatenate(
            [
                ys[r, half * c + span * g : half * c + span * (g + 1), :]
                for r in range(sites)
                for c in range(2)
            ],
            axis=0,
        )
        rows = jnp.dot(place_back, stack, preferred_element_type=F32).astype(BF16)
        placed[group * g : group * (g + 1)] = rows.reshape(group, sites, width)

    relay(sites - 2)
    after_copy = pltpu.make_async_copy(placed, after_ref, local_sem.at[0])
    after_copy.start()
    for r in range(sites - 1):
        relay_far(r)
    relay_all(sites - 1)

    near = [0, -1, 1, -2, 2]
    quads = [(-2, 2), (-1, 1), (0, -3), (3, far)]
    batches = [[far, -3], [3, 2], [-2, 1, -1, 0]]
    ranks = sum(batches, [])
    turn = [0]

    def multiply(offset, q):
        members = [index(b) for b in quads[q]]
        quad = jnp.concatenate(
            [columns[b].reshape(chip_rows * OUTER_CHANNELS, seqs) for b in members], axis=0
        )
        left = chunks[index(offset), :, :OUTER_CHANNELS, :].reshape(pack, seqs)
        buffer = turn[0] % 2
        turn[0] += 1
        product = contract_lanes(quad, left)
        for j in range(2 * chip_rows):
            sums[buffer, PITCH * j : PITCH * j + OUTER_CHANNELS, :] = product[
                OUTER_CHANNELS * j : OUTER_CHANNELS * (j + 1)
            ]
        lanes = slice(pack * index(offset), pack * (index(offset) + 1))
        scale = jnp.concatenate(
            [inverse[chip_rows * b : chip_rows * (b + 1), lanes] for b in members], axis=0
        )
        first = ranks.index(offset) * size * chip_rows + 2 * chip_rows * q
        for e in range(OUTER_CHANNELS):
            rows = sums[buffer, pl.ds(e, 2 * chip_rows, stride=PITCH), :]
            terms[first : first + 2 * chip_rows, e * pack : (e + 1) * pack] = (
                rows * scale
            ).astype(BF16)

    def project(batch):
        count = size * chip_rows
        first = ranks.index(batches[batch][0])
        rows = slice(first * count, (first + len(batches[batch])) * count)
        result = jnp.dot(terms[rows, :], blocks[...], preferred_element_type=F32)
        for k in range(len(batches[batch])):
            for q, members in enumerate(quads):
                for t, b in enumerate(members):
                    row = k * count + (2 * q + t) * chip_rows
                    to = lax.rem(side + b + size, size) * chip_rows
                    to = pl.multiple_of((first + k) * count + to, chip_rows)
                    total[pl.ds(to, chip_rows), :] = result[row : row + chip_rows]
        for at in range(first, first + len(batches[batch])):
            for i in range(sites):
                part = total[at * count : (at + 1) * count, i * PAIR_DIM : (i + 1) * PAIR_DIM]
                part = (part + pair_shift_ref[...]).astype(BF16)
                stage[at, i] = part.reshape(size, chip_rows, PAIR_DIM)

    def deliver(batch):
        for offset in batches[batch]:
            src = stage.at[ranks.index(offset)]
            for c in range(2):

                @pl.when(core == c)
                def _():
                    dst = out_ref.at[:, :, main] if c == 0 else out_ref.at[:, main]
                    if offset:
                        remote(src, dst, 3, out_recv, device(main + offset, side)).start()
                    else:
                        pltpu.make_async_copy(src, dst, local_sem.at[1]).start()

    for r in range(sites):
        for sign in (1, -1):
            ring(r, False, 0, sign, 1).wait_recv()
        for offset in near:
            swap_wait(r, offset)
    for sign in (1, -1):
        ring(sites - 1, False, 0, sign, 2).wait_recv()
    for q in (0, 1):
        for offset in near:
            multiply(offset, q)
    for r in range(sites - 1):
        for step in (1, 2):
            for sign in (1, -1):
                ring(r, False, -2 * sign, sign, step).wait_recv()
    for sign in (1, -1):
        ring(sites - 1, False, 0, sign, 3, True).wait_recv()
    ring(sites - 1, False, 0, 1, far, True).wait_recv()
    for r in range(sites):
        for offset in (-3, 3, far):
            swap_wait(r, offset)
    for batch in range(len(batches)):
        for offset in batches[batch]:
            for q in range(len(quads)):
                if q > 1 or offset not in near:
                    multiply(offset, q)
        project(batch)
        deliver(batch)

    for buffer, send in (
        (chunks.at[pl.ds(0, size - 1)], 0),
        (columns.at[pl.ds(0, size - 1), 0], 1),
        (columns.at[:, 0], 2),
        (stage.at[pl.ds(0, size - 1)], 3),
    ):
        pltpu.make_async_copy(buffer, buffer, sends.at[send]).wait()
    arrived = stage.at[pl.ds(0, size - 1)]
    pltpu.make_async_copy(arrived, arrived, out_recv).wait()
    own = stage.at[ranks.index(0)]
    pltpu.make_async_copy(own, own, local_sem.at[1]).wait()
    after_copy.wait()


def attend_pairs(x, large, small, size):
    seqs, residues = large[0].shape
    part, _, width = x.shape
    chips = size * size
    chip_rows = residues // chips
    sites = chip_rows // 2
    pack = sites * OUTER_CHANNELS
    couple = large[-1]
    count = size * chip_rows
    x = x.reshape(part, chips, chip_rows, width)
    hbm = pl.BlockSpec(memory_space=pl.ANY)
    vmem = pl.BlockSpec(memory_space=pltpu.VMEM)
    dma = pltpu.SemaphoreType.DMA
    return pl.pallas_call(
        functools.partial(core_kernel, size),
        out_shape=(
            jax.ShapeDtypeStruct((seqs, sites, width), BF16),
            jax.ShapeDtypeStruct((sites, size, size, chip_rows, PAIR_DIM), BF16),
        ),
        in_specs=[hbm] * (1 + len(large)) + [vmem] * len(small),
        out_specs=(hbm, hbm),
        scratch_shapes=[
            pltpu.VMEM((2, chips, part, chip_rows, width), BF16),
            *[pltpu.VMEM(a.shape, a.dtype) for a in (large[0], *large[1:])],
            pltpu.VMEM((sites, seqs, width), BF16),
            pltpu.VMEM((sites, seqs, width), BF16),
            pltpu.VMEM((8, seqs), F32),
            pltpu.VMEM((count, size * pack), F32),
            pltpu.VMEM((size, sites, 2 * OUTER_CHANNELS, seqs), BF16),
            pltpu.VMEM((size, 2, sites, OUTER_CHANNELS, seqs), BF16),
            pltpu.VMEM((OUTER_CHANNELS * pack, sites * PAIR_DIM), BF16),
            pltpu.VMEM(couple.shape, F32),
            pltpu.VMEM((2, 2 * chip_rows * PITCH, pack), F32),
            pltpu.VMEM((size * count, OUTER_CHANNELS * pack), BF16),
            pltpu.VMEM((size * count, sites * PAIR_DIM), F32),
            pltpu.VMEM((size, sites, size, chip_rows, PAIR_DIM), BF16),
            pltpu.VMEM((seqs, sites, width), BF16),
            dma((sites, size + 1)),
            dma((sites, size + 1)),
            dma((sites, size)),
            dma,
            dma((4,)),
            dma((3,)),
            dma((5,)),
            dma,
            dma,
            dma((2,)),
        ],
        compiler_params=pltpu.CompilerParams(
            vmem_limit_bytes=VMEM_LIMIT, collective_id=1, has_side_effects=True
        ),
        name="attend_pairs",
    )(x, *large, *small)


def shards(
    homolog_stack_tensor,
    occupancy_indicator,
    chain_existence_flags,
    focus_normal_factor,
    focus_normal_addend,
    probe_index_weights,
    payload_valve_weights,
    logistic_valve_addend,
    focus_exit_weights,
    focus_exit_addend,
    product_mean_layer_stretch,
    product_mean_layer_shift,
    twin_map_matrix,
    twin_map_shift,
    couple_map_matrix,
    couple_map_shift,
):
    seqs, residues = occupancy_indicator.shape
    width = homolog_stack_tensor.shape[-1]
    size = lax.axis_size("dap_0")
    row = lambda v: v[None, :]
    after, pair_rows = attend_pairs(
        homolog_stack_tensor,
        (
            occupancy_indicator,
            probe_index_weights,
            payload_valve_weights,
            focus_exit_weights,
            couple_map_matrix,
        ),
        (
            row(chain_existence_flags),
            row(focus_normal_factor),
            row(focus_normal_addend),
            row(logistic_valve_addend),
            row(focus_exit_addend),
            row(product_mean_layer_stretch),
            row(product_mean_layer_shift),
            twin_map_matrix.T,
            row(twin_map_shift),
            row(couple_map_shift),
        ),
        size,
    )
    return (after, pair_rows.reshape(-1, residues, PAIR_DIM))


def solution(mesh):
    split = Mesh(
        mesh.devices.reshape(mesh.shape["grp"], 8, 8, 2), ("grp", "dap_0", "dap_1", "dap_2")
    )
    return jax.shard_map(
        shards,
        mesh=split,
        in_specs=(
            P(GRP_DAP, None, None),
            P("grp", None),
            P("grp"),
            P(),
            P(),
            P(),
            P(),
            P(),
            P(),
            P(),
            P(),
            P(),
            P(),
            P(),
            P(),
            P(),
        ),
        out_specs=(P("grp", DAP, None), P(GRP_DAP, None, None)),
        check_vma=False,
    )
```

time: 75.7 us -> 71.7 us (0.947)
  Pallas kernels: 72 us -> 68 us
    pallas_call x1 -> x0, Pallas kernels: 36.4 us -> none  [exchange(): pl.pallas_call(functools.partial(exchange_kernel, size), out_shape=jax.Sh...]
    pallas_call x1, Pallas kernels: 35.6 us -> 68 us  [attend_pairs(): pl.pallas_call(functools.partial(core_kernel, size), out_shape=(jax.Shape...]
where the time goes in v5:
time: 71.7 us; the launch traced here: 71.5 us
  Pallas kernels  68 us (95%)
  local copies, waits for them, and re-layouts  2.87 us (4%)
    pallas_call x1, Pallas kernels, attend_pairs(): pl.pallas_call(functools.partial(core_kernel, size), out_shape=(jax.Shape...  68 us
    unnamed x4, local copies, waits for them, and re-layouts  2.87 us

profile of v5, /device:TPU:513, one launch (start us, length us, event | category | flops | bytes accessed | tf_op | source)
XLA Modules:
  0.0 71.5 jit_solution(9197659183802185114)
XLA Ops:
  0.6 68.0 %attend_pairs.1 = (bf16[256,4,256]{2,1,0:T(4,128)(2,1)}, bf16[4,8,8,8,128]{4,3,2,1,0:T(8,128)(2,1)}) custom-call(bf16[2,64,8,256]{3,2,1,0:T(8,128)(2,1)} %bitcast.13, s32[256,512]{1,0:T(8,128)} %present_hbm.1, bf16[256,512]{1,0:T(8,128)(2,1)} %qk_hbm.1, bf16[256,512]{1,0:T(8,128)(2,1)} %vg_hbm.1, bf16[256,256]{1,0:T(8,128)(2,1)} %exit_hbm.1, ...), custom_call_target="tpu_custom_call" | custom-call | tf_op jit(solution)/shard_map/attend_pairs/pallas_call | solution.py:457
  68.6 0.0 copy-start
  68.6 2.1 %copy.20 = bf16[256,4,256]{2,1,0:T(4,128)(2,1)} copy(bf16[256,4,256]{2,1,0:T(4,128)(2,1)} %get-tuple-element.8) | data formatting | bytes 1048576
  70.7 0.0 copy-done
  70.7 0.8 %copy.21 = bf16[4,512,128]{2,1,0:T(8,128)(2,1)} copy(bf16[4,512,128]{2,1,0:T(8,128)(2,1)S(1)} %bitcast.12) | data formatting | bytes 1048576
Async XLA Ops:
  68.6 2.1 %copy-start = (bf16[4,8,8,8,128]{4,3,2,1,0:T(8,128)(2,1)S(1)}, bf16[4,8,8,8,128]{4,3,2,1,0:T(8,128)(2,1)}, u32[]{:S(2)}) copy-start(bf16[4,8,8,8,128]{4,3,2,1,0:T(8,128)(2,1)} %get-tuple-element.5) | copy-start | bytes 1572868

commit v6 on v5

--- a/solution.py
+++ b/solution.py
@@ -47,6 +47,7 @@
     after_ref, out_ref,
     landed, present_ref, qk_ref, vg_ref, exit_ref, couple_ref, xs, ys, keep, inverse, chunks, columns, blocks, wide, sums, terms, total, stage, placed,
     main_recv, side_recv, swap_recv, out_recv, sends, local_sem, load_sem, got, sent, crossed,
+    cross_recv,
 ):
     sites, seqs, width = xs.shape
     residues = present_ref.shape[1]
@@ -76,12 +77,17 @@
     here = y * size + x
     away = lambda d: min(d, size - d)
     steps = [(dy, dx) for dy in range(size) for dx in range(size) if dy or dx]
-    steps.sort(key=lambda d: -(away(d[0]) + away(d[1])))
+    steps.sort(key=lambda d: (-away(d[0]), d[0], -away(d[1])))
     barrier = pltpu.get_barrier_semaphore()
     for dy, dx in steps:
         peer = {"dap_0": lax.rem(y + dy, size), "dap_1": lax.rem(x + dx, size)}
         pl.semaphore_signal(barrier, inc=1, device_id=peer, device_id_type=mesh)
     pl.semaphore_signal(barrier, inc=1, device_id=partner, device_id_type=mesh)
+    for k in range(1, size):
+        for peer in (device(main + k, side), device(main, side + k)):
+            pl.semaphore_signal(
+                barrier, inc=1, device_id={**peer, **partner}, device_id_type=mesh
+            )
     own_rows = pltpu.make_async_copy(
         source_ref.at[:, here], landed.at[core, here], local_sem.at[2]
     )
@@ -100,12 +106,12 @@
     ]
     for load in loads:
         load.start()
-    pl.semaphore_wait(barrier, chips)
+    pl.semaphore_wait(barrier, chips + 2 * (size - 1))
     for dy, dx in steps:
         row, column = lax.rem(y + dy, size), lax.rem(x + dx, size)
         pltpu.make_async_remote_copy(
             src_ref=source_ref.at[:, row * size + column], dst_ref=landed.at[core, here],
-            send_sem=sent, recv_sem=got, device_id={"dap_0": row, "dap_1": column},
+            send_sem=sent, recv_sem=got.at[dy], device_id={"dap_0": row, "dap_1": column},
             device_id_type=mesh,
         ).start()
     for load in loads:
@@ -157,14 +163,23 @@
     counts = jnp.dot(counts, spread, preferred_element_type=F32)
     inverse[...] = 1.0 / jnp.maximum(counts, 1.0)
 
-    others = landed.at[core, pl.ds(0, chips - 1)]
+    def row_of(which, dy, count):
+        first = lax.rem(y - dy + size, size) * size
+        return landed.at[which, pl.ds(first, count)]
+
+    def cross(which, dy):
+        ref = row_of(which, dy, size)
+        return pltpu.make_async_remote_copy(
+            src_ref=ref, dst_ref=ref, send_sem=crossed, recv_sem=cross_recv.at[dy],
+            device_id=partner, device_id_type=mesh,
+        )
+
+    order_of_rows = sorted(range(size), key=lambda dy: (-away(dy), dy))
     own_rows.wait()
-    pltpu.make_async_copy(others, others, got).wait()
-    cross = pltpu.make_async_remote_copy(
-        src_ref=landed.at[core], dst_ref=landed.at[core], send_sem=crossed.at[0],
-        recv_sem=crossed.at[1], device_id=partner, device_id_type=mesh,
-    )
-    cross.start()
+    for dy in order_of_rows:
+        ref = row_of(core, dy, size if dy else size - 1)
+        pltpu.make_async_copy(ref, ref, got.at[dy]).wait()
+        cross(core, dy).start()
 
     span = OUTER_CHANNELS
     pick = one_hot(
@@ -184,8 +199,11 @@
                 xs[r, pl.ds(first, span), :] = rows[span * r : span * (r + 1)]
 
     sort_rows(core)
+    others = landed.at[core, pl.ds(0, chips - 1)]
     pltpu.make_async_copy(others, others, sent).wait()
-    cross.wait()
+    for dy in order_of_rows:
+        cross(1 - core, dy).wait_recv()
+    pltpu.make_async_copy(landed.at[core], landed.at[core], crossed).wait()
     sort_rows(1 - core)
 
     def remote(src, dst, send, recv, target):
@@ -197,72 +215,42 @@
     def index(offset):
         return offset % size
 
-    def ring(r, along_main, origin, sign, step, whole=False):
-        reach = origin - sign * step
-        if along_main:
-            ref = lambda offset: chunks.at[index(offset), r]
-            target, recv, send = device(main + sign * step, side), main_recv, 0
-        else:
-            ref = lambda offset: columns.at[index(offset), core, r]
-            target, recv, send = device(main, side + sign * step), side_recv, 1
-        src, dst = ref(origin), ref(reach)
-        where = index(reach)
-        if abs(reach) == far and not whole:
-            rows = (channels if along_main else OUTER_CHANNELS) // 2
-            first = 0 if sign > 0 else rows
-            src, dst = src.at[pl.ds(first, rows)], dst.at[pl.ds(first, rows)]
-            where = far if sign > 0 else size
-        return remote(src, dst, send, recv.at[r, where], target)
-
-    def swap(r, offset):
+    around = [far, 3, -3, 2, -2, 1, -1]
+
+    def left_to(r, offset):
         return remote(
-            chunks.at[index(offset), r, pl.ds(OUTER_CHANNELS, OUTER_CHANNELS)],
-            columns.at[index(offset), core, r], 2, swap_recv.at[r, index(offset)], partner,
-        )
-
-    def swap_wait(r, offset):
-        ref = columns.at[index(offset), 1 - core, r]
-        remote(ref, ref, 2, swap_recv.at[r, index(offset)], partner).wait_recv()
+            chunks.at[0, r], chunks.at[index(offset), r], 0,
+            main_recv.at[r, index(offset)], device(main - offset, side),
+        )
+
+    def right_to(r, offset):
+        return remote(
+            columns.at[0, core, r], columns.at[index(offset), core, r], 1,
+            side_recv.at[r, index(offset)], device(main, side - offset),
+        )
+
+    def right_across(r, offset, which):
+        target = partner if offset == 0 else {**device(main - offset, side), **partner}
+        return remote(
+            columns.at[0, core, r], columns.at[index(offset), which, r], 2,
+            swap_recv.at[r, index(offset)], target,
+        )
 
     def launch(r):
-        for step in (2, 1):
-            for along_main in (True, False):
-                for sign in (1, -1):
-                    ring(r, along_main, 0, sign, step).start()
-        swap(r, 0).start()
-
-    def launch_all(r):
-        for step in (far, 3, 2, 1):
-            for along_main in (True, False):
-                for sign in (1, -1) if step < far else (1,):
-                    ring(r, along_main, 0, sign, step, True).start()
-        swap(r, 0).start()
-
-    def relay_all(r):
-        for step in (1, 2, 3, far):
-            for sign in (1, -1) if step < far else (1,):
-                ring(r, True, 0, sign, step, True).wait_recv()
-                swap(r, index(-sign * step)).start()
-
-    def relay(r):
-        for along_main in (True, False):
-            for sign in (1, -1):
-                ring(r, along_main, 0, sign, 2).wait_recv()
-                ring(r, along_main, -2 * sign, sign, 2).start()
-                ring(r, along_main, -2 * sign, sign, 1).start()
-                if along_main:
-                    swap(r, -2 * sign).start()
-        for sign in (1, -1):
-            ring(r, True, 0, sign, 1).wait_recv()
-            swap(r, -sign).start()
-
-    def relay_far(r):
-        for sign in (1, -1):
-            ring(r, True, -2 * sign, sign, 1).wait_recv()
-            swap(r, -3 * sign).start()
-        for sign in (1, -1):
-            ring(r, True, -2 * sign, sign, 2).wait_recv()
-        swap(r, far).start()
+        for offset in around:
+            right_to(r, offset).start()
+            right_across(r, offset, core).start()
+        right_across(r, 0, core).start()
+        for offset in around:
+            left_to(r, offset).start()
+
+    def arrive(offsets):
+        for r in range(sites):
+            for offset in offsets:
+                right_across(r, offset, 1 - core).wait_recv()
+                if offset:
+                    right_to(r, offset).wait_recv()
+                    left_to(r, offset).wait_recv()
 
     def one_site(r, carry):
         x = xs[r].astype(F32)
@@ -289,22 +277,11 @@
         after = (x + update).astype(BF16)
         again = normalize(after.astype(F32), gain2_ref[...], offset2_ref[...])
         both = ((contract_lanes(twin_ref[...], again) + shift) * present_row).astype(BF16)
-        chunks[0, r] = both
+        chunks[0, r] = both[:OUTER_CHANNELS]
         columns[0, core, r] = both[OUTER_CHANNELS:]
         ys[r] = after
 
-        @pl.when(r < sites - 1)
-        def _():
-            launch(r)
-
-        @pl.when(r == sites - 1)
-        def _():
-            launch_all(r)
-
-        @pl.when(r >= 2)
-        def _():
-            relay(r - 2)
-
+        launch(r)
         return carry
 
     lax.fori_loop(0, sites, one_site, 0)
@@ -331,12 +308,8 @@
         rows = jnp.dot(place_back, stack, preferred_element_type=F32).astype(BF16)
         placed[group * g : group * (g + 1)] = rows.reshape(group, sites, width)
 
-    relay(sites - 2)
     after_copy = pltpu.make_async_copy(placed, after_ref, local_sem.at[0])
     after_copy.start()
-    for r in range(sites - 1):
-        relay_far(r)
-    relay_all(sites - 1)
 
     near = [0, -1, 1, -2, 2]
     quads = [(-2, 2), (-1, 1), (0, -3), (3, far)]
@@ -349,7 +322,7 @@
         quad = jnp.concatenate(
             [columns[b].reshape(chip_rows * OUTER_CHANNELS, seqs) for b in members], axis=0
         )
-        left = chunks[index(offset), :, :OUTER_CHANNELS, :].reshape(pack, seqs)
+        left = chunks[index(offset)].reshape(pack, seqs)
         buffer = turn[0] % 2
         turn[0] += 1
         product = contract_lanes(quad, left)
@@ -399,26 +372,11 @@
                     else:
                         pltpu.make_async_copy(src, dst, local_sem.at[1]).start()
 
-    for r in range(sites):
-        for sign in (1, -1):
-            ring(r, False, 0, sign, 1).wait_recv()
-        for offset in near:
-            swap_wait(r, offset)
-    for sign in (1, -1):
-        ring(sites - 1, False, 0, sign, 2).wait_recv()
+    arrive(near)
     for q in (0, 1):
         for offset in near:
             multiply(offset, q)
-    for r in range(sites - 1):
-        for step in (1, 2):
-            for sign in (1, -1):
-                ring(r, False, -2 * sign, sign, step).wait_recv()
-    for sign in (1, -1):
-        ring(sites - 1, False, 0, sign, 3, True).wait_recv()
-    ring(sites - 1, False, 0, 1, far, True).wait_recv()
-    for r in range(sites):
-        for offset in (-3, 3, far):
-            swap_wait(r, offset)
+    arrive((-3, 3, far))
     for batch in range(len(batches)):
         for offset in batches[batch]:
             for q in range(len(quads)):
@@ -428,7 +386,7 @@
         deliver(batch)
 
     for buffer, send in (
-        (chunks.at[pl.ds(0, size - 1)], 0),
+        (columns.at[pl.ds(0, size - 1), 0], 0),
         (columns.at[pl.ds(0, size - 1), 0], 1),
         (columns.at[:, 0], 2),
         (stage.at[pl.ds(0, size - 1)], 3),
@@ -469,7 +427,7 @@
             pltpu.VMEM((sites, seqs, width), BF16),
             pltpu.VMEM((8, seqs), F32),
             pltpu.VMEM((count, size * pack), F32),
-            pltpu.VMEM((size, sites, 2 * OUTER_CHANNELS, seqs), BF16),
+            pltpu.VMEM((size, sites, OUTER_CHANNELS, seqs), BF16),
             pltpu.VMEM((size, 2, sites, OUTER_CHANNELS, seqs), BF16),
             pltpu.VMEM((OUTER_CHANNELS * pack, sites * PAIR_DIM), BF16),
             pltpu.VMEM(couple.shape, F32),
@@ -485,15 +443,53 @@
             dma((4,)),
             dma((3,)),
             dma((5,)),
+            dma((size,)),
             dma,
             dma,
-            dma((2,)),
+            dma((size,)),
         ],
         compiler_params=pltpu.CompilerParams(
             vmem_limit_bytes=VMEM_LIMIT, collective_id=1, has_side_effects=True
         ),
         name="attend_pairs",
     )(x, *large, *small)
+
+
+def hand_over_kernel(*refs):
+    count = len(refs) // 4
+    sources, targets, held = refs[:count], refs[count : 2 * count], refs[2 * count : 3 * count]
+    into, out_of = refs[3 * count :][:2]
+    pieces = []
+    for source, target, room in zip(sources, targets, held):
+        for k in range(4):
+            rows = pl.ds(k * source.shape[0] // 4, source.shape[0] // 4)
+            at = len(pieces)
+            pieces.append(
+                (
+                    pltpu.make_async_copy(source.at[rows], room.at[rows], into.at[at]),
+                    pltpu.make_async_copy(room.at[rows], target.at[rows], out_of.at[at]),
+                )
+            )
+    for first, _ in pieces:
+        first.start()
+    for first, second in pieces:
+        first.wait()
+        second.start()
+    for _, second in pieces:
+        second.wait()
+
+
+def hand_over(*arrays):
+    hbm = pl.BlockSpec(memory_space=pl.ANY)
+    return pl.pallas_call(
+        hand_over_kernel,
+        out_shape=tuple(jax.ShapeDtypeStruct(a.shape, a.dtype) for a in arrays),
+        in_specs=[hbm] * len(arrays),
+        out_specs=(hbm,) * len(arrays),
+        scratch_shapes=[pltpu.VMEM(a.shape, a.dtype) for a in arrays]
+        + [pltpu.SemaphoreType.DMA((4 * len(arrays),))] * 2,
+        name="hand_over",
+    )(*arrays)
 
 
 def shards(
@@ -541,7 +537,7 @@
         ),
         size,
     )
-    return (after, pair_rows.reshape(-1, residues, PAIR_DIM))
+    return hand_over(after, pair_rows.reshape(-1, residues, PAIR_DIM))
 
 
 def solution(mesh):

time: 71.7 us -> 76.7 us (1.070)
  Pallas kernels: 68 us -> 75.8 us
  local copies, waits for them, and re-layouts: 2.87 us -> 0 us
    pallas_call x1, Pallas kernels: 68 us -> 73.7 us  [attend_pairs(): pl.pallas_call(functools.partial(core_kernel, size), out_shape=(jax.Shape...]
    unnamed x4 -> x0, local copies, waits for them, and re-layouts: 2.87 us -> none
    pallas_call x0 -> x1, Pallas kernels: none -> 2.09 us  [hand_over(): pl.pallas_call(hand_over_kernel, out_shape=tuple((jax.ShapeDtypeStruct(a....]
where the time goes in v6:
time: 76.7 us; the launch traced here: 76.5 us
  Pallas kernels  75.8 us (99%)
    pallas_call x1, Pallas kernels, attend_pairs(): pl.pallas_call(functools.partial(core_kernel, size), out_shape=(jax.Shape...  73.7 us
    pallas_call x1, Pallas kernels, hand_over(): pl.pallas_call(hand_over_kernel, out_shape=tuple((jax.ShapeDtypeStruct(a....  2.09 us

profile of v6, /device:TPU:513, one launch (start us, length us, event | category | flops | bytes accessed | tf_op | source)
XLA Modules:
  0.0 76.5 jit_solution(12336206213485122399)
XLA Ops:
  0.6 73.7 %attend_pairs.1 = (bf16[256,4,256]{2,1,0:T(4,128)(2,1)}, bf16[4,8,8,8,128]{4,3,2,1,0:T(8,128)(2,1)}) custom-call(bf16[2,64,8,256]{3,2,1,0:T(8,128)(2,1)} %bitcast.13, s32[256,512]{1,0:T(8,128)} %present_hbm.1, bf16[256,512]{1,0:T(8,128)(2,1)} %qk_hbm.1, bf16[256,512]{1,0:T(8,128)(2,1)} %vg_hbm.1, bf16[256,256]{1,0:T(8,128)(2,1)} %exit_hbm.1, ...), custom_call_target="tpu_custom_call" | custom-call | tf_op jit(solution)/shard_map/attend_pairs/pallas_call | solution.py:415
  74.4 2.1 %hand_over.1 = (bf16[256,4,256]{2,1,0:T(4,128)(2,1)}, bf16[4,512,128]{2,1,0:T(8,128)(2,1)}) custom-call(bf16[256,4,256]{2,1,0:T(4,128)(2,1)} %get-tuple-element.4.refs_0_, bf16[4,512,128]{2,1,0:T(8,128)(2,1)} %bitcast.12), custom_call_target="tpu_custom_call" | custom-call | tf_op jit(solution)/shard_map/hand_over/pallas_call | solution.py:484

commit v7 on v6

--- a/solution.py
+++ b/solution.py
@@ -47,7 +47,6 @@
     after_ref, out_ref,
     landed, present_ref, qk_ref, vg_ref, exit_ref, couple_ref, xs, ys, keep, inverse, chunks, columns, blocks, wide, sums, terms, total, stage, placed,
     main_recv, side_recv, swap_recv, out_recv, sends, local_sem, load_sem, got, sent, crossed,
-    cross_recv,
 ):
     sites, seqs, width = xs.shape
     residues = present_ref.shape[1]
@@ -77,17 +76,12 @@
     here = y * size + x
     away = lambda d: min(d, size - d)
     steps = [(dy, dx) for dy in range(size) for dx in range(size) if dy or dx]
-    steps.sort(key=lambda d: (-away(d[0]), d[0], -away(d[1])))
+    steps.sort(key=lambda d: -(away(d[0]) + away(d[1])))
     barrier = pltpu.get_barrier_semaphore()
     for dy, dx in steps:
         peer = {"dap_0": lax.rem(y + dy, size), "dap_1": lax.rem(x + dx, size)}
         pl.semaphore_signal(barrier, inc=1, device_id=peer, device_id_type=mesh)
     pl.semaphore_signal(barrier, inc=1, device_id=partner, device_id_type=mesh)
-    for k in range(1, size):
-        for peer in (device(main + k, side), device(main, side + k)):
-            pl.semaphore_signal(
-                barrier, inc=1, device_id={**peer, **partner}, device_id_type=mesh
-            )
     own_rows = pltpu.make_async_copy(
         source_ref.at[:, here], landed.at[core, here], local_sem.at[2]
     )
@@ -106,12 +100,12 @@
     ]
     for load in loads:
         load.start()
-    pl.semaphore_wait(barrier, chips + 2 * (size - 1))
+    pl.semaphore_wait(barrier, chips)
     for dy, dx in steps:
         row, column = lax.rem(y + dy, size), lax.rem(x + dx, size)
         pltpu.make_async_remote_copy(
             src_ref=source_ref.at[:, row * size + column], dst_ref=landed.at[core, here],
-            send_sem=sent, recv_sem=got.at[dy], device_id={"dap_0": row, "dap_1": column},
+            send_sem=sent, recv_sem=got, device_id={"dap_0": row, "dap_1": column},
             device_id_type=mesh,
         ).start()
     for load in loads:
@@ -163,23 +157,14 @@
     counts = jnp.dot(counts, spread, preferred_element_type=F32)
     inverse[...] = 1.0 / jnp.maximum(counts, 1.0)
 
-    def row_of(which, dy, count):
-        first = lax.rem(y - dy + size, size) * size
-        return landed.at[which, pl.ds(first, count)]
-
-    def cross(which, dy):
-        ref = row_of(which, dy, size)
-        return pltpu.make_async_remote_copy(
-            src_ref=ref, dst_ref=ref, send_sem=crossed, recv_sem=cross_recv.at[dy],
-            device_id=partner, device_id_type=mesh,
-        )
-
-    order_of_rows = sorted(range(size), key=lambda dy: (-away(dy), dy))
+    others = landed.at[core, pl.ds(0, chips - 1)]
     own_rows.wait()
-    for dy in order_of_rows:
-        ref = row_of(core, dy, size if dy else size - 1)
-        pltpu.make_async_copy(ref, ref, got.at[dy]).wait()
-        cross(core, dy).start()
+    pltpu.make_async_copy(others, others, got).wait()
+    cross = pltpu.make_async_remote_copy(
+        src_ref=landed.at[core], dst_ref=landed.at[core], send_sem=crossed.at[0],
+        recv_sem=crossed.at[1], device_id=partner, device_id_type=mesh,
+    )
+    cross.start()
 
     span = OUTER_CHANNELS
     pick = one_hot(
@@ -199,11 +184,8 @@
                 xs[r, pl.ds(first, span), :] = rows[span * r : span * (r + 1)]
 
     sort_rows(core)
-    others = landed.at[core, pl.ds(0, chips - 1)]
     pltpu.make_async_copy(others, others, sent).wait()
-    for dy in order_of_rows:
-        cross(1 - core, dy).wait_recv()
-    pltpu.make_async_copy(landed.at[core], landed.at[core], crossed).wait()
+    cross.wait()
     sort_rows(1 - core)
 
     def remote(src, dst, send, recv, target):
@@ -215,42 +197,58 @@
     def index(offset):
         return offset % size
 
-    around = [far, 3, -3, 2, -2, 1, -1]
-
-    def left_to(r, offset):
-        return remote(
-            chunks.at[0, r], chunks.at[index(offset), r], 0,
-            main_recv.at[r, index(offset)], device(main - offset, side),
-        )
-
-    def right_to(r, offset):
-        return remote(
-            columns.at[0, core, r], columns.at[index(offset), core, r], 1,
-            side_recv.at[r, index(offset)], device(main, side - offset),
-        )
-
-    def right_across(r, offset, which):
-        target = partner if offset == 0 else {**device(main - offset, side), **partner}
-        return remote(
-            columns.at[0, core, r], columns.at[index(offset), which, r], 2,
-            swap_recv.at[r, index(offset)], target,
-        )
+    def hop(r, way, origin, sign, step, cross=False):
+        reach = origin - sign * step
+        if way == 0:
+            ref = lambda offset: chunks.at[index(offset), r]
+            target = device(main + sign * step, side)
+        else:
+            which = core if way == 1 or cross else 1 - core
+            ref = lambda offset: columns.at[index(offset), which, r]
+            target = device(main, side + sign * step)
+            if cross:
+                target = {**device(main + sign * step, side), **partner}
+        src, dst = ref(origin), ref(reach)
+        where = index(reach)
+        if abs(reach) == far:
+            rows = OUTER_CHANNELS // 2
+            first = pl.ds(0 if sign > 0 else rows, rows)
+            src, dst = src.at[first], dst.at[first]
+            where = far if sign > 0 else size
+        return remote(src, dst, way, (main_recv, side_recv, swap_recv)[way].at[r, where], target)
+
+    def swap(r, which):
+        ref = columns.at[0, which, r]
+        return remote(ref, ref, 2, swap_recv.at[r, 0], partner)
 
     def launch(r):
-        for offset in around:
-            right_to(r, offset).start()
-            right_across(r, offset, core).start()
-        right_across(r, 0, core).start()
-        for offset in around:
-            left_to(r, offset).start()
-
-    def arrive(offsets):
-        for r in range(sites):
-            for offset in offsets:
-                right_across(r, offset, 1 - core).wait_recv()
-                if offset:
-                    right_to(r, offset).wait_recv()
-                    left_to(r, offset).wait_recv()
+        for step in (2, 1):
+            for sign in (1, -1):
+                hop(r, 1, 0, sign, step).start()
+                hop(r, 2, 0, sign, step, True).start()
+        swap(r, core).start()
+        for step in (2, 1):
+            for sign in (1, -1):
+                hop(r, 0, 0, sign, step).start()
+
+    def relay(r):
+        for way in (1, 2, 0):
+            for sign in (1, -1):
+                hop(r, way, 0, sign, 2).wait_recv()
+                hop(r, way, -2 * sign, sign, 2).start()
+                hop(r, way, -2 * sign, sign, 1).start()
+
+    def arrive_near(r):
+        swap(r, 1 - core).wait_recv()
+        for way in (1, 2, 0):
+            for sign in (1, -1):
+                hop(r, way, 0, sign, 1).wait_recv()
+
+    def arrive_far(r):
+        for way in (1, 2, 0):
+            for step in (1, 2):
+                for sign in (1, -1):
+                    hop(r, way, -2 * sign, sign, step).wait_recv()
 
     def one_site(r, carry):
         x = xs[r].astype(F32)
@@ -282,6 +280,11 @@
         ys[r] = after
 
         launch(r)
+
+        @pl.when(r >= 2)
+        def _():
+            relay(r - 2)
+
         return carry
 
     lax.fori_loop(0, sites, one_site, 0)
@@ -308,8 +311,10 @@
         rows = jnp.dot(place_back, stack, preferred_element_type=F32).astype(BF16)
         placed[group * g : group * (g + 1)] = rows.reshape(group, sites, width)
 
+    relay(sites - 2)
     after_copy = pltpu.make_async_copy(placed, after_ref, local_sem.at[0])
     after_copy.start()
+    relay(sites - 1)
 
     near = [0, -1, 1, -2, 2]
     quads = [(-2, 2), (-1, 1), (0, -3), (3, far)]
@@ -372,11 +377,13 @@
                     else:
                         pltpu.make_async_copy(src, dst, local_sem.at[1]).start()
 
-    arrive(near)
+    for r in range(sites):
+        arrive_near(r)
     for q in (0, 1):
         for offset in near:
             multiply(offset, q)
-    arrive((-3, 3, far))
+    for r in range(sites):
+        arrive_far(r)
     for batch in range(len(batches)):
         for offset in batches[batch]:
             for q in range(len(quads)):
@@ -438,15 +445,14 @@
             pltpu.VMEM((seqs, sites, width), BF16),
             dma((sites, size + 1)),
             dma((sites, size + 1)),
-            dma((sites, size)),
+            dma((sites, size + 1)),
             dma,
             dma((4,)),
             dma((3,)),
             dma((5,)),
-            dma((size,)),
             dma,
             dma,
-            dma((size,)),
+            dma((2,)),
         ],
         compiler_params=pltpu.CompilerParams(
             vmem_limit_bytes=VMEM_LIMIT, collective_id=1, has_side_effects=True

time: 76.7 us -> 66.9 us (0.87)
  Pallas kernels: 75.8 us -> 66 us
    pallas_call x1, Pallas kernels: 73.7 us -> 64 us  [attend_pairs(): pl.pallas_call(functools.partial(core_kernel, size), out_shape=(jax.Shape...]
where the time goes in v7:
time: 66.9 us; the launch traced here: 66.7 us
  Pallas kernels  66 us (99%)
    pallas_call x1, Pallas kernels, attend_pairs(): pl.pallas_call(functools.partial(core_kernel, size), out_shape=(jax.Shape...  64 us
    pallas_call x1, Pallas kernels, hand_over(): pl.pallas_call(hand_over_kernel, out_shape=tuple((jax.ShapeDtypeStruct(a....  2.09 us

profile of v7, /device:TPU:513, one launch (start us, length us, event | category | flops | bytes accessed | tf_op | source)
XLA Modules:
  0.0 66.7 jit_solution(10194515934343259996)
XLA Ops:
  0.6 64.0 %attend_pairs.1 = (bf16[256,4,256]{2,1,0:T(4,128)(2,1)}, bf16[4,8,8,8,128]{4,3,2,1,0:T(8,128)(2,1)}) custom-call(bf16[2,64,8,256]{3,2,1,0:T(8,128)(2,1)} %bitcast.13, s32[256,512]{1,0:T(8,128)} %present_hbm.1, bf16[256,512]{1,0:T(8,128)(2,1)} %qk_hbm.1, bf16[256,512]{1,0:T(8,128)(2,1)} %vg_hbm.1, bf16[256,256]{1,0:T(8,128)(2,1)} %exit_hbm.1, ...), custom_call_target="tpu_custom_call" | custom-call | tf_op jit(solution)/shard_map/attend_pairs/pallas_call | solution.py:422
  64.6 2.1 %hand_over.1 = (bf16[256,4,256]{2,1,0:T(4,128)(2,1)}, bf16[4,512,128]{2,1,0:T(8,128)(2,1)}) custom-call(bf16[256,4,256]{2,1,0:T(4,128)(2,1)} %get-tuple-element.4.refs_0_, bf16[4,512,128]{2,1,0:T(8,128)(2,1)} %bitcast.12), custom_call_target="tpu_custom_call" | custom-call | tf_op jit(solution)/shard_map/hand_over/pallas_call | solution.py:490

commit v8 on v7

--- a/solution.py
+++ b/solution.py
@@ -45,7 +45,7 @@
     offset_ref, gate_ref, exit_add_ref, gain2_ref, offset2_ref, twin_ref, shift_ref,
     pair_shift_ref,
     after_ref, out_ref,
-    landed, present_ref, qk_ref, vg_ref, exit_ref, couple_ref, xs, ys, keep, inverse, chunks, columns, blocks, wide, sums, terms, total, stage, placed,
+    source, landed, present_ref, qk_ref, vg_ref, exit_ref, couple_ref, xs, ys, keep, inverse, chunks, columns, blocks, wide, sums, terms, total, stage, placed,
     main_recv, side_recv, swap_recv, out_recv, sends, local_sem, load_sem, got, sent, crossed,
 ):
     sites, seqs, width = xs.shape
@@ -90,6 +90,7 @@
         pltpu.make_async_copy(a, b, load_sem.at[i])
         for i, (a, b) in enumerate(
             (
+                (source_ref, source),
                 (present_hbm, present_ref),
                 (couple_hbm, couple_ref),
                 (qk_hbm, qk_ref),
@@ -101,14 +102,15 @@
     for load in loads:
         load.start()
     pl.semaphore_wait(barrier, chips)
+    loads[0].wait()
     for dy, dx in steps:
         row, column = lax.rem(y + dy, size), lax.rem(x + dx, size)
         pltpu.make_async_remote_copy(
-            src_ref=source_ref.at[:, row * size + column], dst_ref=landed.at[core, here],
+            src_ref=source.at[:, row * size + column], dst_ref=landed.at[core, here],
             send_sem=sent, recv_sem=got, device_id={"dap_0": row, "dap_1": column},
             device_id_type=mesh,
         ).start()
-    for load in loads:
+    for load in loads[1:]:
         load.wait()
 
     half = seqs // 2
@@ -322,29 +324,30 @@
     ranks = sum(batches, [])
     turn = [0]
 
-    def multiply(offset, q):
+    def multiply(pair, q):
         members = [index(b) for b in quads[q]]
         quad = jnp.concatenate(
             [columns[b].reshape(chip_rows * OUTER_CHANNELS, seqs) for b in members], axis=0
         )
-        left = chunks[index(offset)].reshape(pack, seqs)
-        buffer = turn[0] % 2
+        left = jnp.concatenate([chunks[index(o)].reshape(pack, seqs) for o in pair], axis=0)
+        product = contract_lanes(quad, left)
         turn[0] += 1
-        product = contract_lanes(quad, left)
-        for j in range(2 * chip_rows):
-            sums[buffer, PITCH * j : PITCH * j + OUTER_CHANNELS, :] = product[
-                OUTER_CHANNELS * j : OUTER_CHANNELS * (j + 1)
-            ]
-        lanes = slice(pack * index(offset), pack * (index(offset) + 1))
-        scale = jnp.concatenate(
-            [inverse[chip_rows * b : chip_rows * (b + 1), lanes] for b in members], axis=0
-        )
-        first = ranks.index(offset) * size * chip_rows + 2 * chip_rows * q
-        for e in range(OUTER_CHANNELS):
-            rows = sums[buffer, pl.ds(e, 2 * chip_rows, stride=PITCH), :]
-            terms[first : first + 2 * chip_rows, e * pack : (e + 1) * pack] = (
-                rows * scale
-            ).astype(BF16)
+        for k, offset in enumerate(pair):
+            buffer = 2 * (turn[0] % 2) + k
+            for j in range(2 * chip_rows):
+                sums[buffer, PITCH * j : PITCH * j + OUTER_CHANNELS, :] = product[
+                    OUTER_CHANNELS * j : OUTER_CHANNELS * (j + 1), pack * k : pack * (k + 1)
+                ]
+            lanes = slice(pack * index(offset), pack * (index(offset) + 1))
+            scale = jnp.concatenate(
+                [inverse[chip_rows * b : chip_rows * (b + 1), lanes] for b in members], axis=0
+            )
+            first = ranks.index(offset) * size * chip_rows + 2 * chip_rows * q
+            for e in range(OUTER_CHANNELS):
+                rows = sums[buffer, pl.ds(e, 2 * chip_rows, stride=PITCH), :]
+                terms[first : first + 2 * chip_rows, e * pack : (e + 1) * pack] = (
+                    rows * scale
+                ).astype(BF16)
 
     def project(batch):
         count = size * chip_rows
@@ -379,16 +382,18 @@
 
     for r in range(sites):
         arrive_near(r)
+    pairs = [tuple(batch[k : k + 2]) for batch in batches for k in range(0, len(batch), 2)]
+    early = [pair for pair in pairs if all(offset in near for offset in pair)]
     for q in (0, 1):
-        for offset in near:
-            multiply(offset, q)
+        for pair in early:
+            multiply(pair, q)
     for r in range(sites):
         arrive_far(r)
     for batch in range(len(batches)):
-        for offset in batches[batch]:
+        for pair in pairs:
             for q in range(len(quads)):
-                if q > 1 or offset not in near:
-                    multiply(offset, q)
+                if pair[0] in batches[batch] and (q > 1 or pair not in early):
+                    multiply(pair, q)
         project(batch)
         deliver(batch)
 
@@ -428,6 +433,7 @@
         in_specs=[hbm] * (1 + len(large)) + [vmem] * len(small),
         out_specs=(hbm, hbm),
         scratch_shapes=[
+            pltpu.VMEM(x.shape, BF16),
             pltpu.VMEM((2, chips, part, chip_rows, width), BF16),
             *[pltpu.VMEM(a.shape, a.dtype) for a in (large[0], *large[1:])],
             pltpu.VMEM((sites, seqs, width), BF16),
@@ -438,7 +444,7 @@
             pltpu.VMEM((size, 2, sites, OUTER_CHANNELS, seqs), BF16),
             pltpu.VMEM((OUTER_CHANNELS * pack, sites * PAIR_DIM), BF16),
             pltpu.VMEM(couple.shape, F32),
-            pltpu.VMEM((2, 2 * chip_rows * PITCH, pack), F32),
+            pltpu.VMEM((4, 2 * chip_rows * PITCH, pack), F32),
             pltpu.VMEM((size * count, OUTER_CHANNELS * pack), BF16),
             pltpu.VMEM((size * count, sites * PAIR_DIM), F32),
             pltpu.VMEM((size, sites, size, chip_rows, PAIR_DIM), BF16),
@@ -449,7 +455,7 @@
             dma,
             dma((4,)),
             dma((3,)),
-            dma((5,)),
+            dma((6,)),
             dma,
             dma,
             dma((2,)),

time: 66.9 us -> 66.7 us (level)
  no operation moved by 1% of the time
where the time goes in v8:
time: 66.7 us; the launch traced here: 66.5 us
  Pallas kernels  65.8 us (99%)
    pallas_call x1, Pallas kernels, attend_pairs(): pl.pallas_call(functools.partial(core_kernel, size), out_shape=(jax.Shape...  63.7 us
    pallas_call x1, Pallas kernels, hand_over(): pl.pallas_call(hand_over_kernel, out_shape=tuple((jax.ShapeDtypeStruct(a....  2.09 us

profile of v8, /device:TPU:513, one launch (start us, length us, event | category | flops | bytes accessed | tf_op | source)
XLA Modules:
  0.0 66.5 jit_solution(169714630756327760)
XLA Ops:
  0.6 63.7 %attend_pairs.1 = (bf16[256,4,256]{2,1,0:T(4,128)(2,1)}, bf16[4,8,8,8,128]{4,3,2,1,0:T(8,128)(2,1)}) custom-call(bf16[2,64,8,256]{3,2,1,0:T(8,128)(2,1)} %bitcast.13, s32[256,512]{1,0:T(8,128)} %present_hbm.1, bf16[256,512]{1,0:T(8,128)(2,1)} %qk_hbm.1, bf16[256,512]{1,0:T(8,128)(2,1)} %vg_hbm.1, bf16[256,256]{1,0:T(8,128)(2,1)} %exit_hbm.1, ...), custom_call_target="tpu_custom_call" | custom-call | tf_op jit(solution)/shard_map/attend_pairs/pallas_call | solution.py:427
  64.4 2.1 %hand_over.1 = (bf16[256,4,256]{2,1,0:T(4,128)(2,1)}, bf16[4,512,128]{2,1,0:T(8,128)(2,1)}) custom-call(bf16[256,4,256]{2,1,0:T(4,128)(2,1)} %get-tuple-element.4.refs_0_, bf16[4,512,128]{2,1,0:T(8,128)(2,1)} %bitcast.12), custom_call_target="tpu_custom_call" | custom-call | tf_op jit(solution)/shard_map/hand_over/pallas_call | solution.py:496
